TPU v7x, 16 devices: a whole 2x2x2 slice. The times are simulated.
16 devices in a mesh: ep: 16 (over z, y, x, core).
Axes of the slice: x: 2, y: 2, z: 2, core: 2. Of those that a mesh axis runs over, the one named last changes fastest.
Arguments:
- tokens: bfloat16 [8192, 2048], P('ep')
- expert_idx: int32 [8192], P('ep')
- w_router: bfloat16 [2048, 64], replicated
- w_in: bfloat16 [64, 2048, 1408], P('ep')
- w_out: bfloat16 [64, 1408, 2048], P('ep')
- loss_probe: bfloat16 [8192, 2048], P('ep')
Outputs:
- output 1: float32 [], replicated
- output 2: bfloat16 [8192, 2048], P('ep')
- output 3: bfloat16 [64, 2048, 1408], P('ep')
- output 4: bfloat16 [64, 1408, 2048], P('ep')
- output 5: float32 [2048, 64], replicated
All inputs are finite; a program needn't handle non-finite values.
Results may differ from a plain program's by a relative error of at most 0.00525.
Values are sent between devices in bfloat16 or wider.
A program may use at most 1 GiB of HBM per device.

v0:
```python
import jax
import jax.numpy as jnp
from jax import lax
from jax.sharding import PartitionSpec as P

AUX_WEIGHT = 0.01


def solution(mesh):
    groups = mesh.shape['ep']

    def local_step(tokens, expert_idx, w_router, w_in, w_out, loss_probe):
        tok_count, hidden_dim = tokens.shape
        local_experts = w_in.shape[0]
        num_experts = w_router.shape[1]
        all_tokens = tok_count * groups
        capacity = (5 * all_tokens + 4 * num_experts - 1) // (4 * num_experts)
        pair_max = 2 * tok_count // num_experts
        send_rows = num_experts * pair_max
        grad_scale = 1.0 / (all_tokens * hidden_dim)
        buf_shape = (num_experts, pair_max, hidden_dim)
        recv_shape = (groups, local_experts, pair_max, hidden_dim)
        my_index = lax.axis_index('ep')
        expert_ids = jnp.arange(num_experts, dtype=jnp.int32)
        onehot = (expert_idx[:, None] == expert_ids[None, :]).astype(jnp.int32)
        all_counts = lax.all_gather(jnp.sum(onehot, axis=0), 'ep')
        earlier = (jnp.arange(groups) < my_index).astype(jnp.int32)
        offsets = jnp.sum(earlier[:, None] * all_counts, axis=0)
        totals = jnp.sum(all_counts, axis=0)
        before = jnp.cumsum(onehot, axis=0) - onehot
        local_rank = jnp.sum(onehot * before, axis=1)
        position = local_rank + jnp.sum(onehot * offsets[None, :], axis=1)
        keep_mask = position < capacity
        slot_index = jnp.where(keep_mask, expert_idx * pair_max + local_rank, send_rows)
        source = jax.ops.segment_sum(jnp.arange(tok_count, dtype=jnp.int32) + 1, slot_index, num_segments=send_rows + 1)[:send_rows] - 1
        filled = (source >= 0)[:, None]
        src_safe = jnp.maximum(source, 0)
        slot_safe = jnp.minimum(slot_index, send_rows - 1)

        send_x = jnp.where(filled, jnp.take(tokens, src_safe, axis=0), 0).reshape(buf_shape)
        recv_x = lax.all_to_all(send_x, 'ep', 0, 0, tiled=True).reshape(recv_shape)
        pre_act = jnp.einsum('sekh,ehf->sekf', recv_x, w_in, preferred_element_type=jnp.float32)
        hidden = jnp.maximum(pre_act, 0.0).astype(jnp.bfloat16)
        z_rows = jnp.einsum('sekf,efh->sekh', hidden, w_out, preferred_element_type=jnp.float32).astype(jnp.bfloat16)
        back_z = lax.all_to_all(z_rows.reshape(buf_shape), 'ep', 0, 0, tiled=True)
        z_tok = jnp.where(keep_mask[:, None], jnp.take(back_z.reshape(send_rows, hidden_dim), slot_safe, axis=0), 0).astype(jnp.float32)

        logits = jnp.dot(tokens, w_router, preferred_element_type=jnp.float32)
        router_prob = jax.nn.softmax(logits, axis=-1)
        hot_f = onehot.astype(jnp.float32)
        gate_prob = jnp.sum(hot_f * router_prob, axis=1)
        keep_f = keep_mask.astype(jnp.float32)
        probe_f = loss_probe.astype(jnp.float32)
        y_part = jnp.sum((tokens.astype(jnp.float32) + (keep_f * gate_prob)[:, None] * z_tok) * probe_f)
        global_stats = lax.psum(jnp.concatenate([jnp.sum(router_prob, axis=0), y_part[None]]), 'ep')
        route_frac = totals.astype(jnp.float32) / all_tokens
        prob_mean = global_stats[:num_experts] / all_tokens
        loss_value = global_stats[num_experts] * grad_scale + AUX_WEIGHT * num_experts * jnp.sum(route_frac * prob_mean)

        g_tok = ((keep_f * gate_prob * grad_scale)[:, None] * probe_f).astype(jnp.bfloat16)
        send_g = jnp.where(filled, jnp.take(g_tok, src_safe, axis=0), 0).reshape(buf_shape)
        recv_g = lax.all_to_all(send_g, 'ep', 0, 0, tiled=True).reshape(recv_shape)
        d_w_out = jnp.einsum('sekf,sekh->efh', hidden, recv_g, preferred_element_type=jnp.float32).astype(jnp.bfloat16)
        grad_hidden = jnp.einsum('sekh,efh->sekf', recv_g, w_out, preferred_element_type=jnp.float32)
        grad_pre = jnp.where(hidden > 0, grad_hidden, 0.0).astype(jnp.bfloat16)
        d_w_in = jnp.einsum('sekh,sekf->ehf', recv_x, grad_pre, preferred_element_type=jnp.float32).astype(jnp.bfloat16)
        u_rows = jnp.einsum('sekf,ehf->sekh', grad_pre, w_in, preferred_element_type=jnp.float32).astype(jnp.bfloat16)
        back_u = lax.all_to_all(u_rows.reshape(buf_shape), 'ep', 0, 0, tiled=True)
        u_tok = jnp.where(keep_mask[:, None], jnp.take(back_u.reshape(send_rows, hidden_dim), slot_safe, axis=0), 0).astype(jnp.float32)

        d_gate = keep_f * grad_scale * jnp.sum(probe_f * z_tok, axis=1)
        d_logit_task = (d_gate * gate_prob)[:, None] * (hot_f - router_prob)
        aux_coef = AUX_WEIGHT * num_experts * route_frac / all_tokens
        d_logit_aux = router_prob * (aux_coef[None, :] - jnp.sum(router_prob * aux_coef[None, :], axis=1, keepdims=True))
        d_logit = (d_logit_task + d_logit_aux).astype(jnp.bfloat16)
        d_w_router = lax.psum(jnp.einsum('th,te->he', tokens, d_logit, preferred_element_type=jnp.float32), 'ep')
        dx_router = jnp.einsum('te,he->th', d_logit, w_router, preferred_element_type=jnp.float32)
        d_tokens = (grad_scale * probe_f + u_tok + dx_router).astype(jnp.bfloat16)
        return loss_value, d_tokens, d_w_in, d_w_out, d_w_router

    in_specs = (P('ep', None), P('ep'), P(None, None), P('ep', None, None), P('ep', None, None), P('ep', None))
    out_specs = (P(), P('ep', None), P('ep', None, None), P('ep', None, None), P(None, None))
    return jax.shard_map(local_step, mesh=mesh, in_specs=in_specs, out_specs=out_specs, check_vma=False)
```

profile of v0, /device:TPU:0, one launch (start us, length us, event | category | flops | bytes accessed | tf_op | source)
XLA Modules:
  0.0 444.1 jit_solution(9949653769041400937)
XLA Ops:
  7.2 0.0 copy-start
  7.2 0.0 copy-start.1
  7.2 0.9 convert_reduce_fusion
  8.2 0.2 dynamic-update-slice
  8.4 34.7 %all-reduce = s32[1024]{0:T(1024)S(1)} all-reduce(s32[1024]{0:T(1024)S(1)} %dynamic-update-slice), channel_id=2, replica_groups=mesh['ep'=16] {'ep'}, use_global_device_ids=true, to_apply=%add | all-reduce | flops 1024 | bytes 8192
  43.1 0.1 reshape.156
  43.2 0.1 fusion.52
  43.3 0.7 fusion.41
  44.0 1.2 reduce-window.6
  45.2 0.2 slice_reduce_fusion
  45.5 0.0 copy-done
  45.5 2.4 fusion.53
  47.9 0.9 multiply_reduce_fusion
  48.8 0.8 select_reduce_fusion
  49.6 0.7 compare_and_fusion
  50.3 4.1 scatter_custom_fusion
  54.5 6.0 %gather_fusion = bf16[1024,2048]{1,0:T(8,128)(2,1)} fusion(bf16[512,2048]{1,0:T(8,128)(2,1)S(1)} %copy-done.1, s32[1024]{0:T(1024)S(1)} %maximum_clamp_fusion), kind=kCustom, calls=%fused_computation.clone | custom fusion | bytes 8392704 | tf_op jit(solution)/shard_map/jit(_take)/gather | solution.py:40
  60.4 2.7 select_select_fusion.1
  63.2 53.1 %all_to_all.20 = bf16[64,16,2048]{2,1,0:T(8,128)(2,1)S(1)} all-to-all(bf16[64,16,2048]{2,1,0:T(8,128)(2,1)S(1)} %bitcast.72), channel_id=1, replica_groups=mesh['ep'=16] {'ep'}, dimensions={0} | all-to-all | bytes 8388608 | tf_op jit(solution)/shard_map/all_to_all | solution.py:41
  116.2 12.8 %fusion.27 = bf16[16,4,16,1408]{3,2,0,1:T(8,128)(2,1)S(1)} fusion(bf16[4,2048,1408]{2,1,0:T(8,128)(2,1)} %param.13, bf16[16,4,16,2048]{3,2,1,0:T(8,128)(2,1)S(1)} %bitcast.75), kind=kOutput, calls=%fused_computation.37 | convolution fusion | flops 5908463616 | bytes 30146560 | tf_op jit(solution)/shard_map/sekh,ehf->sekf/dot_general | solution.py:42
  129.0 0.0 copy-start.24
  129.0 12.6 %convert_bitcast_fusion.1 = bf16[16,4,16,2048]{3,2,0,1:T(8,128)(2,1)S(1)} fusion(bf16[16,4,16,1408]{3,2,0,1:T(8,128)(2,1)S(1)} %fusion.27, bf16[4,1408,2048]{2,1,0:T(8,128)(2,1)} %param.14), kind=kOutput, calls=%fused_computation.34 | convolution fusion | flops 5907677184 | bytes 30146560 | tf_op jit(solution)/shard_map/sekf,efh->sekh/dot_general | solution.py:44
  141.6 2.5 copy.27
  144.1 3.4 all-to-all-start.1
  147.6 53.5 %all-to-all-done.1 = bf16[64,16,2048]{2,1,0:T(8,128)(2,1)} async-done(((bf16[64,16,2048]{2,1,0:T(8,128)(2,1)}), bf16[64,16,2048]{2,1,0:T(8,128)(2,1)}, u32[]{:S(2)}, u32[]{:S(2)}) %all-to-all-start.1) | async-done | bytes 4194336 | tf_op jit(solution)/shard_map/all_to_all | solution.py:45
  201.1 8.0 %gather_fusion.1 = bf16[512,2048]{1,0:T(8,128)(2,1)} fusion(bf16[1024,2048]{1,0:T(8,128)(2,1)} %bitcast.11, s32[1024]{0:T(1024)S(1)} %pad_clamp_fusion), kind=kCustom, calls=%fused_computation.1.clone | custom fusion | bytes 4196352 | tf_op jit(solution)/shard_map/jit(_take)/gather | solution.py:46
  209.1 6.2 %fusion.19 = (f32[512]{0:T(512)S(1)}, f32[]{:T(128)}, bf16[512,2048]{1,0:T(8,128)(2,1)}) fusion(bf16[512,2048]{1,0:T(8,128)(2,1)} %param.15, bf16[512,2048]{1,0:T(8,128)(2,1)} %gather_fusion.1, pred[512]{0:T(512)(128)(4,1)S(1)} %get-tuple-element.19, pred[512]{0:T(512)(128)(4,1)S(1)} %get-tuple-element.18, f32[512]{0:T(512)S(1)} %get-tuple-element.17, ...), kind=kLoop, calls=%fused_computation.29 | loop fusion | flops 13630975 | bytes 8395780 | tf_op jit(solution)/shard_map/reduce_sum | solution.py:71
  215.2 10.7 %gather_fusion.2 = bf16[1024,2048]{1,0:T(8,128)(2,1)} fusion(bf16[512,2048]{1,0:T(8,128)(2,1)} %get-tuple-element.21, s32[1024]{0:T(1024)S(1)} %maximum_clamp_fusion), kind=kCustom, calls=%fused_computation.2.clone | custom fusion | bytes 8392704 | tf_op jit(solution)/shard_map/jit(_take)/gather | solution.py:61
  225.9 4.1 select_select_fusion
  230.0 4.2 all-to-all-start.2
  234.2 0.0 all-reduce.3.cloned.1.call-start
  234.3 1.3 convolution_bitcast_fusion
  235.6 0.0 all-reduce.3.cloned.1.call-update
  235.7 0.7 pad_maximum_fusion
  236.4 79.6 %psum.14 = f32[65]{0:T(128)S(1)} all-reduce(f32[65]{0:T(128)S(1)} %pad_maximum_fusion), channel_id=1, replica_groups=mesh['ep'=16] {'ep'}, use_global_device_ids=true, to_apply=%region_12.15 | all-reduce | flops 65 | bytes 520 | tf_op jit(solution)/shard_map/psum | solution.py:55
  316.0 0.6 slice.18
  316.6 0.6 multiply_reduce_fusion.2
  318.5 0.0 all-to-all-done.2
  318.5 13.5 %bitcast_convert_fusion = bf16[4,1408,2048]{2,1,0:T(8,128)(2,1)} fusion(bf16[16,4,16,1408]{3,2,0,1:T(8,128)(2,1)} %copy-done.24, bf16[16,4,16,2048]{3,2,1,0:T(8,128)(2,1)} %bitcast.15), kind=kOutput, calls=%fused_computation.5 | convolution fusion | flops 5917114368 | bytes 30146560 | tf_op jit(solution)/shard_map/sekf,sekh->efh/dot_general | solution.py:63
  332.0 14.1 %fusion.8 = bf16[16,4,16,1408]{3,2,0,1:T(8,128)(2,1)} fusion(bf16[16,4,16,1408]{3,2,0,1:T(8,128)(2,1)} %copy-done.24, bf16[4,1408,2048]{2,1,0:T(8,128)(2,1)} %param.14, bf16[16,4,16,2048]{3,2,1,0:T(8,128)(2,1)} %bitcast.15), kind=kOutput, calls=%fused_computation.20 | convolution fusion | flops 5909905408 | bytes 33030144 | tf_op jit(solution)/shard_map/sekh,efh->sekf/dot_general | solution.py:64
  346.1 13.4 %convert_bitcast_fusion = bf16[16,4,16,2048]{3,2,0,1:T(8,128)(2,1)} fusion(bf16[16,4,16,1408]{3,2,0,1:T(8,128)(2,1)} %fusion.8, bf16[4,2048,1408]{2,1,0:T(8,128)(2,1)} %param.13), kind=kOutput, calls=%fused_computation.33 | convolution fusion | flops 5907677184 | bytes 30146560 | tf_op jit(solution)/shard_map/sekf,ehf->sekh/dot_general | solution.py:67
  359.5 4.7 %copy.29 = bf16[16,4,16,2048]{3,2,1,0:T(8,128)(2,1)} copy(bf16[16,4,16,2048]{3,2,0,1:T(8,128)(2,1)} %convert_bitcast_fusion) | data formatting | bytes 8388608 | tf_op jit(solution)/shard_map/convert_element_type | solution.py:67
  364.3 3.9 all-to-all-start.3
  368.2 14.2 %bitcast_convert_fusion.1 = bf16[4,2048,1408]{2,1,0:T(8,128)(2,1)} fusion(bf16[16,4,16,2048]{3,2,1,0:T(8,128)(2,1)} %bitcast.76, bf16[16,4,16,1408]{3,2,0,1:T(8,128)(2,1)} %fusion.8), kind=kOutput, calls=%fused_computation.6 | convolution fusion | flops 5917114368 | bytes 30146560 | tf_op jit(solution)/shard_map/sekh,sekf->ehf/dot_general | solution.py:66
  382.4 39.3 %all-to-all-done.3 = bf16[64,16,2048]{2,1,0:T(8,128)(2,1)} async-done(((bf16[64,16,2048]{2,1,0:T(8,128)(2,1)}), bf16[64,16,2048]{2,1,0:T(8,128)(2,1)}, u32[]{:S(2)}, u32[]{:S(2)}) %all-to-all-start.3) | async-done | bytes 4194336 | tf_op jit(solution)/shard_map/all_to_all | solution.py:68
  421.7 8.1 %gather_fusion.3 = bf16[512,2048]{1,0:T(8,128)(2,1)} fusion(bf16[1024,2048]{1,0:T(8,128)(2,1)} %bitcast.21, s32[1024]{0:T(1024)S(1)} %copy-done.13), kind=kCustom, calls=%fused_computation.3.clone | custom fusion | bytes 4196352 | tf_op jit(solution)/shard_map/jit(_take)/gather | solution.py:69
  429.9 4.3 fusion.17
  434.2 1.9 copy.49
  (60 shorter events, 0.2 us)
Async XLA Ops:
  7.2 38.3 %copy-start = (bf16[2048,64]{0,1:T(8,128)(2,1)S(1)}, bf16[2048,64]{0,1:T(8,128)(2,1)}, u32[]{:S(2)}) copy-start(bf16[2048,64]{0,1:T(8,128)(2,1)} %param.12) | copy-start | bytes 786436
  7.2 47.3 %copy-start.1 = (bf16[512,2048]{1,0:T(8,128)(2,1)S(1)}, bf16[512,2048]{1,0:T(8,128)(2,1)}, u32[]{:S(2)}) copy-start(bf16[512,2048]{1,0:T(8,128)(2,1)} %param.10) | copy-start | bytes 6291460
  43.3 191.0 %copy-start.22 = (f32[64]{0:T(128)}, f32[64]{0:T(128)S(1)}, u32[]{:S(2)}) copy-start(f32[64]{0:T(128)S(1)} %convert_multiply_fusion.5) | copy-start | bytes 772
  47.8 186.4 %copy-start.4 = (f32[512,64]{0,1:T(8,128)}, f32[512,64]{0,1:T(8,128)S(1)}, u32[]{:S(2)}) copy-start(f32[512,64]{0,1:T(8,128)S(1)} %get-tuple-element.25) | copy-start | bytes 393220
  47.8 186.4 %copy-start.8 = (f32[512]{0:T(512)}, f32[512]{0:T(512)S(1)}, u32[]{:S(2)}) copy-start(f32[512]{0:T(512)S(1)} %get-tuple-element.24) | copy-start | bytes 6148
  47.9 186.4 %copy-start.10 = (f32[512]{0:T(512)}, f32[512]{0:T(512)S(1)}, u32[]{:S(2)}) copy-start(f32[512]{0:T(512)S(1)} %fusion.43) | copy-start | bytes 6148
  48.8 185.5 %copy-start.16 = (f32[512]{0:T(512)}, f32[512]{0:T(512)S(1)}, u32[]{:S(2)}) copy-start(f32[512]{0:T(512)S(1)} %get-tuple-element.9) | copy-start | bytes 6148
  49.6 184.6 %copy-start.14 = (pred[512]{0:T(512)(128)(4,1)}, pred[512]{0:T(512)(128)(4,1)S(1)}, u32[]{:S(2)}) copy-start(pred[512]{0:T(512)(128)(4,1)S(1)} %get-tuple-element.18) | copy-start | bytes 1540
  50.3 158.8 %copy-start.20 = (pred[512]{0:T(512)(128)(4,1)}, pred[512]{0:T(512)(128)(4,1)S(1)}, u32[]{:S(2)}) copy-start(pred[512]{0:T(512)(128)(4,1)S(1)} %get-tuple-element.19) | copy-start | bytes 1540
  116.2 12.8 %copy-start.2 = (bf16[64,16,2048]{2,1,0:T(8,128)(2,1)}, bf16[64,16,2048]{2,1,0:T(8,128)(2,1)S(1)}, u32[]{:S(2)}) copy-start(bf16[64,16,2048]{2,1,0:T(8,128)(2,1)S(1)} %all_to_all.20) | copy-start | bytes 12582916
  129.0 12.6 %copy-start.24 = (bf16[16,4,16,1408]{3,2,0,1:T(8,128)(2,1)}, bf16[16,4,16,1408]{3,2,0,1:T(8,128)(2,1)S(1)}, u32[]{:S(2)}) copy-start(bf16[16,4,16,1408]{3,2,0,1:T(8,128)(2,1)S(1)} %fusion.27) | copy-start | bytes 8650756
  144.1 57.0 %all-to-all-start.1 = ((bf16[64,16,2048]{2,1,0:T(8,128)(2,1)}), bf16[64,16,2048]{2,1,0:T(8,128)(2,1)}, u32[]{:S(2)}, u32[]{:S(2)}) async-start(bf16[64,16,2048]{2,1,0:T(8,128)(2,1)} %bitcast.73), calls=%async_computation.1 | async-start | bytes 8388608 | tf_op jit(solution)/shard_map/all_to_all | solution.py:45
  147.6 61.5 %copy-start.12 = (s32[1024]{0:T(1024)}, s32[1024]{0:T(1024)S(1)}, u32[]{:S(2)}) copy-start(s32[1024]{0:T(1024)S(1)} %pad_clamp_fusion) | copy-start | bytes 12292
  230.0 4.3 copy-start.6
  230.0 88.5 %all-to-all-start.2 = ((bf16[64,16,2048]{2,1,0:T(8,128)(2,1)}), bf16[64,16,2048]{2,1,0:T(8,128)(2,1)}, u32[]{:S(2)}, u32[]{:S(2)}) async-start(bf16[64,16,2048]{2,1,0:T(8,128)(2,1)} %bitcast.71), calls=%async_computation.2 | async-start | bytes 8388608 | tf_op jit(solution)/shard_map/all_to_all | solution.py:62
  234.2 200.0 %all-reduce.3.cloned.1.call-start = ((), (), s32[]{:S(2)}) async-start(), calls=%async_computation.4 | async-start | bytes 1048576 | tf_op jit(solution)/shard_map/psum | solution.py:76
  234.2 97.7 %copy-start.18 = (f32[512]{0:T(512)}, f32[512]{0:T(512)S(1)}, u32[]{:S(2)}) copy-start(f32[512]{0:T(512)S(1)} %multiply_multiply_fusion) | copy-start | bytes 6148
  364.3 57.4 %all-to-all-start.3 = ((bf16[64,16,2048]{2,1,0:T(8,128)(2,1)}), bf16[64,16,2048]{2,1,0:T(8,128)(2,1)}, u32[]{:S(2)}, u32[]{:S(2)}) async-start(bf16[64,16,2048]{2,1,0:T(8,128)(2,1)} %bitcast.74), calls=%async_computation.3 | async-start | bytes 8388608 | tf_op jit(solution)/shard_map/all_to_all | solution.py:68
  368.2 53.5 %copy-start.13 = (s32[1024]{0:T(1024)S(1)}, s32[1024]{0:T(1024)}, u32[]{:S(2)}) copy-start(s32[1024]{0:T(1024)} %copy-done.12) | copy-start | bytes 12292
  421.7 8.2 %copy-start.3 = (bf16[512,2048]{1,0:T(8,128)(2,1)S(1)}, bf16[512,2048]{1,0:T(8,128)(2,1)}, u32[]{:S(2)}) copy-start(bf16[512,2048]{1,0:T(8,128)(2,1)} %param.15) | copy-start | bytes 6291460
  421.7 8.2 %copy-start.5 = (f32[512,64]{0,1:T(8,128)S(1)}, f32[512,64]{0,1:T(8,128)}, u32[]{:S(2)}) copy-start(f32[512,64]{0,1:T(8,128)} %copy-done.4) | copy-start | bytes 393220
  421.7 8.2 %copy-start.7 = (s32[512]{0:T(512)S(1)}, s32[512]{0:T(512)}, u32[]{:S(2)}) copy-start(s32[512]{0:T(512)} %param.11) | copy-start | bytes 6148
  421.7 8.2 %copy-start.9 = (f32[512]{0:T(512)S(1)}, f32[512]{0:T(512)}, u32[]{:S(2)}) copy-start(f32[512]{0:T(512)} %copy-done.8) | copy-start | bytes 6148
  421.7 8.2 %copy-start.11 = (f32[512]{0:T(512)S(1)}, f32[512]{0:T(512)}, u32[]{:S(2)}) copy-start(f32[512]{0:T(512)} %copy-done.10) | copy-start | bytes 6148
  421.7 8.2 %copy-start.15 = (pred[512]{0:T(512)(128)(4,1)S(1)}, pred[512]{0:T(512)(128)(4,1)}, u32[]{:S(2)}) copy-start(pred[512]{0:T(512)(128)(4,1)} %copy-done.14) | copy-start | bytes 1540
  421.7 8.2 %copy-start.17 = (f32[512]{0:T(512)S(1)}, f32[512]{0:T(512)}, u32[]{:S(2)}) copy-start(f32[512]{0:T(512)} %copy-done.16) | copy-start | bytes 6148
  421.7 8.2 %copy-start.19 = (f32[512]{0:T(512)S(1)}, f32[512]{0:T(512)}, u32[]{:S(2)}) copy-start(f32[512]{0:T(512)} %copy-done.18) | copy-start | bytes 6148
  421.7 8.2 %copy-start.21 = (pred[512]{0:T(512)(128)(4,1)S(1)}, pred[512]{0:T(512)(128)(4,1)}, u32[]{:S(2)}) copy-start(pred[512]{0:T(512)(128)(4,1)} %copy-done.20) | copy-start | bytes 1540
  421.7 8.2 %copy-start.23 = (f32[64]{0:T(128)S(1)}, f32[64]{0:T(128)}, u32[]{:S(2)}) copy-start(f32[64]{0:T(128)} %copy-done.22) | copy-start | bytes 772
Sparse Core Ops, SparseCore 0:
  239.9 87.4 all-reduce.2
where the time goes:
time: 445 us; the launch traced here: 444 us
  blocking collectives  167 us (38%)
  waiting for transfers between devices  92.8 us (21%)
  matrix products  88.5 us (20%)
  local copies, waits for them, and re-layouts  43.1 us (10%)
  other arithmetic  23.9 us (5%)
  between operations  16.9 us (4%)
  starting transfers between devices  11.5 us (3%)
    psum x1, blocking collectives, local_step(): lax.psum(jnp.concatenate([jnp.sum(router_prob, axis=0), y_part[None]]), '...  79.6 us
    all_to_all x1, waiting for transfers between devices, local_step(): back_z = lax.all_to_all(z_rows.reshape(buf_shape), 'ep', 0, 0, tiled=True)  53.5 us
    all_to_all x1, blocking collectives, local_step(): recv_x = lax.all_to_all(send_x, 'ep', 0, 0, tiled=True).reshape(recv_shape)  53.1 us
    all_to_all x1, waiting for transfers between devices, local_step(): back_u = lax.all_to_all(u_rows.reshape(buf_shape), 'ep', 0, 0, tiled=True)  39.3 us
    unnamed x1, blocking collectives  34.7 us
    dot_general x1, matrix products, local_step(): jnp.einsum('sekh,sekf->ehf', recv_x, grad_pre, preferred_element_type=jnp...  14.2 us
    dot_general x1, matrix products, local_step(): jnp.einsum('sekh,efh->sekf', recv_g, w_out, preferred_element_type=jnp.fl...  14.1 us
    dot_general x1, matrix products, local_step(): jnp.einsum('sekf,sekh->efh', hidden, recv_g, preferred_element_type=jnp.f...  13.5 us
  transfers between devices with their start and end apart: 4, of which 2 were waited for; matrix products, arithmetic and copies ran while one was open for 17% of the time, Pallas kernels for 0%

commit v1 on v0

v1 whole, which is shorter than its diff:
```python
import functools

import jax
import jax.numpy as jnp
from jax import lax
from jax.experimental import pallas as pl
from jax.experimental.pallas import tpu as pltpu
from jax.sharding import PartitionSpec as P

AUX_WEIGHT = 0.01
LANES = 128
MESH = pl.DeviceIdType.MESH
F32 = jnp.float32
BF16 = jnp.bfloat16
ORDER = (8, 4, 2, 12, 10, 6, 14, 9, 5, 3, 13, 11, 7, 15, 1)
VMEM = pl.BlockSpec(memory_space=pltpu.VMEM)
HBM = pl.BlockSpec(memory_space=pl.ANY)
HI = lax.Precision.HIGHEST
NT = (((1,), (1,)), ((), ()))
TN = (((0,), (0,)), ((), ()))


def dot(a, b, dims=(((1,), (0,)), ((), ())), **kw):
    return lax.dot_general(a, b, dims, preferred_element_type=F32, **kw)


def iota(shape, axis):
    return lax.broadcasted_iota(jnp.int32, shape, axis)


def greet(me, groups):
    barrier = pltpu.get_barrier_semaphore()
    for k in range(1, groups):
        pl.semaphore_signal(barrier, inc=1, device_id=(me ^ k,), device_id_type=MESH)
    pl.semaphore_wait(barrier, groups - 1)


def route_kernel(pair_max, idx_ref, x_ref, wr_ref, p_ref, meta_ref, msg_ref):
    experts, tok = p_ref.shape
    idx = idx_ref[...]
    onehot = (iota((experts, tok), 0) == idx).astype(F32)
    upper = (iota((tok, tok), 0) < iota((tok, tok), 1)).astype(BF16)
    before = dot(onehot.astype(BF16), upper)
    rank = jnp.sum(onehot * before, axis=0, keepdims=True)
    logits = dot(wr_ref[...], x_ref[...], NT)
    e = jnp.exp(logits - jnp.max(logits, axis=0, keepdims=True))
    p = e / jnp.sum(e, axis=0, keepdims=True)
    p_ref[...] = p
    gate = jnp.sum(onehot * p, axis=0, keepdims=True)
    rank_hot = (iota((LANES, tok), 0) == rank.astype(jnp.int32)).astype(F32)
    table = dot(onehot * gate, rank_hot, NT, precision=HI)
    count = jnp.sum(onehot, axis=1, keepdims=True)
    lane = iota((experts, LANES), 1)
    row = jnp.where(lane == pair_max, count, jnp.where(lane == pair_max + 1, jnp.sum(p, axis=1, keepdims=True), table))
    msg_ref[...] = row
    meta_ref[0:1, :] = idx * pair_max + rank.astype(jnp.int32)
    meta_ref[1:2, :] = rank.astype(jnp.int32)
    meta_ref[2:, :] = jnp.zeros((meta_ref.shape[0] - 2, tok), jnp.int32)


def pack_kernel(meta_ref, x_ref, r_ref, xs_ref, rs_ref):
    rows, tok = xs_ref.shape[0], x_ref.shape[0]
    base = pl.program_id(0) * rows
    pick = ((iota((rows, tok), 0) + base) == meta_ref[0:1, :]).astype(BF16)
    xs_ref[...] = dot(pick, x_ref[...]).astype(BF16)
    rs_ref[...] = dot(pick, r_ref[...]).astype(BF16)


def expert_kernel(groups, capacity, scale, msg_ref, xs_ref, rs_ref, w1_ref, w2_ref,
                  x_out, h_out, g_out, q_out, u_out, stat_out, rz_out,
                  xbuf, rbuf, mbuf, zsend, zbuf, send, recv, msend, mrecv, zss, zrs, own, xsem):
    e = pl.program_id(0)
    last = pl.num_programs(0) - 1
    me = lax.axis_index('ep')
    pair = xbuf.shape[2]
    hidden = xbuf.shape[3]
    experts = mbuf.shape[1]
    local = xbuf.shape[0]

    def msg_copy(k):
        d = me ^ k
        return pltpu.make_async_remote_copy(
            src_ref=msg_ref, dst_ref=mbuf.at[me], send_sem=msend.at[k], recv_sem=mrecv.at[me],
            device_id=(d,), device_id_type=MESH)

    def msg_got(k):
        d = me ^ k
        return pltpu.make_async_remote_copy(
            src_ref=msg_ref, dst_ref=mbuf.at[d], send_sem=msend.at[k], recv_sem=mrecv.at[d],
            device_id=(d,), device_id_type=MESH)

    def row_copy(t, c, k, src_dev):
        d = me ^ k
        src, buf = ((xs_ref, xbuf), (rs_ref, rbuf))[t]
        return pltpu.make_async_remote_copy(
            src_ref=src.at[d, c], dst_ref=buf.at[c, src_dev], send_sem=send.at[t, c, k],
            recv_sem=recv.at[t, c, src_dev], device_id=(d,), device_id_type=MESH)

    def own_copy(t, c):
        src, buf = ((xs_ref, xbuf), (rs_ref, rbuf))[t]
        return pltpu.make_async_copy(src.at[me, c], buf.at[c, me], own.at[t, c])

    own_msg = pltpu.make_async_copy(msg_ref, mbuf.at[me], mrecv.at[me])

    @pl.when(e == 0)
    def _():
        greet(me, groups)
        own_msg.start()
        for k in ORDER:
            msg_copy(k).start()

        def chunk(c, _):
            for t in range(2):
                own_copy(t, c).start()
                for k in ORDER:
                    row_copy(t, c, k, me).start()
            return 0
        lax.fori_loop(0, local, chunk, 0)
        own_msg.wait()
        for k in ORDER:
            msg_got(k).wait_recv()

    rows = groups * pair
    gates, offs = [], []
    off = jnp.zeros((1, LANES), F32)
    for s in range(groups):
        row = mbuf[s, pl.ds(me * local + e, 1), :]
        gates.append(jnp.broadcast_to(row, (pair, LANES)))
        offs.append(jnp.broadcast_to(off, (pair, LANES)))
        off = off + row
    slot = lax.rem(iota((rows, LANES), 0), pair)
    lane = iota((rows, LANES), 1)
    gate = jnp.sum(jnp.where(lane == slot, jnp.concatenate(gates, axis=0), 0.0), axis=1, keepdims=True)
    ahead = jnp.sum(jnp.where(lane == pair, jnp.concatenate(offs, axis=0), 0.0), axis=1, keepdims=True)
    place = ahead + lax.rem(iota((rows, 1), 0), pair).astype(F32)
    keep = (place < float(capacity)).astype(F32)

    own_copy(0, e).wait()
    for k in ORDER:
        row_copy(0, e, k, me ^ k).wait_recv()
    x_save = pltpu.make_async_copy(xbuf.at[e], x_out.at[e], xsem)
    x_save.start()
    x = xbuf[e].reshape(rows, hidden)
    h = jnp.maximum(dot(x, w1_ref[0]), 0.0).astype(BF16)
    h_out[0] = h
    z = dot(h, w2_ref[0]).astype(BF16).astype(F32)
    own_copy(1, e).wait()
    for k in ORDER:
        row_copy(1, e, k, me ^ k).wait_recv()
    r = rbuf[e].reshape(rows, hidden).astype(F32)
    g = ((keep * gate * scale) * r).astype(BF16)
    g_out[0] = g
    rz = keep * jnp.sum(r * z, axis=1, keepdims=True)
    rz_rows = jnp.sum(jnp.where(lane == slot, rz, 0.0).reshape(groups, pair, LANES), axis=1)
    for s in range(groups):
        zsend[s, pl.ds(e, 1), :] = rz_rows[s:s + 1, :]
    dh = dot(g, w2_ref[0], NT)
    q = jnp.where(h.astype(F32) > 0.0, dh, 0.0).astype(BF16)
    q_out[0] = q
    u_out[...] = dot(q, w1_ref[0], NT).astype(BF16).reshape(groups, 1, pair, hidden)
    x_save.wait()

    @pl.when(e == last)
    def _():
        def z_copy(k, src_dev):
            d = me ^ k
            return pltpu.make_async_remote_copy(
                src_ref=zsend.at[d], dst_ref=zbuf.at[src_dev], send_sem=zss.at[k], recv_sem=zrs.at[src_dev],
                device_id=(d,), device_id_type=MESH)
        mine = pltpu.make_async_copy(zsend.at[me], zbuf.at[me], zrs.at[me])
        mine.start()
        for k in ORDER:
            z_copy(k, me).start()
        for k in ORDER:
            msg_copy(k).wait_send()

        def chunk(c, _):
            for t in range(2):
                for k in ORDER:
                    row_copy(t, c, k, me).wait_send()
            return 0
        lax.fori_loop(0, local, chunk, 0)
        mine.wait()
        for k in ORDER:
            z_copy(k, me ^ k).wait_recv()
        for k in ORDER:
            z_copy(k, me).wait_send()
        stat_out[...] = mbuf[...]
        rz_out[...] = zbuf[...]


def weight_kernel(x_ref, h_ref, g_ref, q_ref, d1_ref, d2_ref):
    d1_ref[0] = dot(x_ref[0], q_ref[0], TN).astype(BF16)
    d2_ref[0] = dot(h_ref[0], g_ref[0], TN).astype(BF16)


def router_kernel(groups, pair, scale, all_tokens, idx_ref, meta_ref, p_ref, stat_ref, rz_ref, x_ref, r_ref,
                  l_out, w_out, loss_out, part, got, red, lsend, lgot, s1, r1, s2, r2, s3, r3):
    me = lax.axis_index('ep')
    greet(me, groups)
    experts, tok = p_ref.shape
    local = experts // groups
    onehot = (iota((experts, tok), 0) == idx_ref[...]).astype(F32)
    rank_hot = iota((LANES, tok), 0) == meta_ref[1:2, :]
    p = p_ref[...]
    gate = jnp.sum(onehot * p, axis=0, keepdims=True)
    table = jnp.concatenate([rz_ref[d, 0:local, :] for d in range(groups)], axis=0)
    rz_all = dot(table, onehot, TN, precision=HI)
    rz = jnp.sum(jnp.where(rank_hot, rz_all, 0.0), axis=0, keepdims=True)
    stat = jnp.zeros((experts, LANES), F32)
    for d in range(groups):
        stat = stat + stat_ref[d]
    lane = iota((experts, LANES), 1)
    total = jnp.sum(jnp.where(lane == pair, stat, 0.0), axis=1, keepdims=True)
    psum = jnp.sum(jnp.where(lane == pair + 1, stat, 0.0), axis=1, keepdims=True)
    frac = total / float(all_tokens)
    aux = AUX_WEIGHT * experts * jnp.sum(frac * (psum / float(all_tokens)), axis=0, keepdims=True)
    coef = (AUX_WEIGHT * experts / all_tokens) * frac
    d_gate = scale * rz
    d_task = (d_gate * gate) * (onehot - p)
    d_aux = p * (coef - jnp.sum(p * coef, axis=0, keepdims=True))
    l = (d_task + d_aux).astype(BF16)
    l_out[...] = l
    for d in range(groups):
        part[d] = dot(l, x_ref[:, d * LANES:(d + 1) * LANES])

    def rs_copy(k, src_dev):
        d = me ^ k
        return pltpu.make_async_remote_copy(
            src_ref=part.at[d], dst_ref=got.at[src_dev], send_sem=s1.at[k], recv_sem=r1.at[src_dev],
            device_id=(d,), device_id_type=MESH)

    def ls_copy(k, src_dev):
        d = me ^ k
        return pltpu.make_async_remote_copy(
            src_ref=lsend, dst_ref=lgot.at[src_dev], send_sem=s3.at[k], recv_sem=r3.at[src_dev],
            device_id=(d,), device_id_type=MESH)

    def ag_copy(k, src_dev):
        d = me ^ k
        return pltpu.make_async_remote_copy(
            src_ref=red, dst_ref=w_out.at[src_dev], send_sem=s2.at[k], recv_sem=r2.at[src_dev],
            device_id=(d,), device_id_type=MESH)

    for k in ORDER:
        rs_copy(k, me).start()
    xr = jnp.sum(jnp.sum(x_ref[...].astype(F32) * r_ref[...].astype(F32), axis=0, keepdims=True), axis=1, keepdims=True)
    mine = xr + jnp.sum(gate * rz, axis=1, keepdims=True)
    lsend[...] = jnp.broadcast_to(mine, lsend.shape)
    for k in ORDER:
        ls_copy(k, me).start()
    for k in ORDER:
        rs_copy(k, me ^ k).wait_recv()
    got[me] = part[me]
    total_w = jnp.zeros(red.shape, F32)
    for d in range(groups):
        total_w = total_w + got[d]
    red[...] = total_w
    for k in ORDER:
        ag_copy(k, me).start()
    for k in ORDER:
        ls_copy(k, me ^ k).wait_recv()
    lgot[me] = lsend[...]
    y = jnp.zeros(lsend.shape, F32)
    for d in range(groups):
        y = y + lgot[d]
    loss_out[...] = y * scale + aux
    w_out[me] = total_w
    for k in ORDER:
        ag_copy(k, me ^ k).wait_recv()
    for k in ORDER:
        rs_copy(k, me).wait_send()
        ls_copy(k, me).wait_send()
        ag_copy(k, me).wait_send()


def token_kernel(scale, meta_ref, u_ref, r_ref, l_ref, wr_ref, o_ref):
    slots, tok = u_ref.shape[0], r_ref.shape[0]
    pick = (iota((slots, tok), 0) == meta_ref[0:1, :]).astype(BF16)
    u = dot(pick, u_ref[...], TN)
    dx = dot(l_ref[...], wr_ref[...], TN)
    o_ref[...] = (scale * r_ref[...].astype(F32) + u + dx).astype(BF16)


def params(**kw):
    return pltpu.CompilerParams(vmem_limit_bytes=62 * 2 ** 20, **kw)


def solution(mesh):
    groups = mesh.shape['ep']

    def local_step(tokens, expert_idx, w_router, w_in, w_out, loss_probe):
        tok, hidden = tokens.shape
        local, _, ffn = w_in.shape
        experts = w_router.shape[1]
        all_tokens = tok * groups
        capacity = (5 * all_tokens + 4 * experts - 1) // (4 * experts)
        pair = 2 * tok // experts
        slots = experts * pair
        rows = groups * pair
        scale = 1.0 / (all_tokens * hidden)
        sds = jax.ShapeDtypeStruct
        idx = expert_idx.reshape(1, tok)
        wr_t = w_router.T

        p_t, meta, msg = pl.pallas_call(
            functools.partial(route_kernel, pair),
            out_shape=[sds((experts, tok), F32), sds((8, tok), jnp.int32), sds((experts, LANES), F32)],
            in_specs=[VMEM] * 3, out_specs=[VMEM] * 3, name='route',
            compiler_params=params())(idx, tokens, wr_t)

        steps = 4
        full = lambda shape: pl.BlockSpec(shape, lambda i: (0,) * len(shape))
        xs, rs = pl.pallas_call(
            pack_kernel, grid=(steps,),
            out_shape=[sds((slots, hidden), BF16)] * 2,
            in_specs=[full((8, tok)), full((tok, hidden)), full((tok, hidden))],
            out_specs=[pl.BlockSpec((slots // steps, hidden), lambda i: (i, 0))] * 2, name='pack',
            compiler_params=params())(meta, tokens, loss_probe)

        per = lambda shape: pl.BlockSpec((1,) + shape, lambda i: (i,) + (0,) * len(shape))
        dma = pltpu.SemaphoreType.DMA
        shape4 = (groups, local, pair, hidden)
        x_buf, h_buf, g_buf, q_buf, u_rows, stat, rz = pl.pallas_call(
            functools.partial(expert_kernel, groups, capacity, scale), grid=(local,),
            out_shape=[sds((local, groups, pair, hidden), BF16), sds((local, rows, ffn), BF16), sds((local, rows, hidden), BF16),
                       sds((local, rows, ffn), BF16), sds(shape4, BF16), sds((groups, experts, LANES), F32), sds((groups, 8, LANES), F32)],
            in_specs=[VMEM, HBM, HBM, per((hidden, ffn)), per((ffn, hidden))],
            out_specs=[HBM, per((rows, ffn)), per((rows, hidden)), per((rows, ffn)),
                       pl.BlockSpec((groups, 1, pair, hidden), lambda i: (0, i, 0, 0)),
                       full((groups, experts, LANES)), full((groups, 8, LANES))],
            scratch_shapes=[pltpu.VMEM((local, groups, pair, hidden), BF16), pltpu.VMEM((local, groups, pair, hidden), BF16),
                            pltpu.VMEM((groups, experts, LANES), F32), pltpu.VMEM((groups, 8, LANES), F32),
                            pltpu.VMEM((groups, 8, LANES), F32), dma((2, local, groups)), dma((2, local, groups)),
                            dma((groups,)), dma((groups,)), dma((groups,)), dma((groups,)), dma((2, local)), dma(())],
            name='experts',
            compiler_params=params(collective_id=0, has_side_effects=True))(
                msg, xs.reshape(shape4), rs.reshape(shape4), w_in, w_out)

        u_back = lax.all_to_all(u_rows, 'ep', 0, 0, tiled=True).reshape(slots, hidden)

        d_w_in, d_w_out = pl.pallas_call(
            weight_kernel, grid=(local,),
            out_shape=[sds((local, hidden, ffn), BF16), sds((local, ffn, hidden), BF16)],
            in_specs=[per((rows, hidden)), per((rows, ffn)), per((rows, hidden)), per((rows, ffn))],
            out_specs=[per((hidden, ffn)), per((ffn, hidden))], name='weights',
            cost_estimate=pl.CostEstimate(flops=4 * local * rows * hidden * ffn, bytes_accessed=50_000_000, transcendentals=0),
            compiler_params=params())(x_buf.reshape(local, rows, hidden), h_buf, g_buf, q_buf)

        l_t, d_wr, loss = pl.pallas_call(
            functools.partial(router_kernel, groups, pair, scale, all_tokens),
            out_shape=[sds((experts, tok), BF16), sds((groups, experts, LANES), F32), sds((8, LANES), F32)],
            in_specs=[VMEM] * 7, out_specs=[VMEM] * 3,
            scratch_shapes=[pltpu.VMEM((groups, experts, LANES), F32), pltpu.VMEM((groups, experts, LANES), F32),
                            pltpu.VMEM((experts, LANES), F32), pltpu.VMEM((8, LANES), F32), pltpu.VMEM((groups, 8, LANES), F32)]
            + [dma((groups,))] * 6, name='router',
            cost_estimate=pl.CostEstimate(flops=30_000_000_000, bytes_accessed=8_000_000, transcendentals=0),
            compiler_params=params(collective_id=1, has_side_effects=True))(
                idx, meta, p_t, stat, rz, tokens, loss_probe)

        cols = hidden // steps
        col = lambda r: pl.BlockSpec((r, cols), lambda i: (0, i))
        d_tokens = pl.pallas_call(
            functools.partial(token_kernel, scale), grid=(steps,),
            out_shape=sds((tok, hidden), BF16),
            in_specs=[full((8, tok)), col(slots), col(tok), full((experts, tok)), col(experts)],
            out_specs=col(tok), name='tokens',
            compiler_params=params())(meta, u_back, loss_probe, l_t, wr_t)

        d_w_router = d_wr.transpose(0, 2, 1).reshape(hidden, experts)
        return loss[0, 0], d_tokens, d_w_in, d_w_out, d_w_router

    in_specs = (P('ep', None), P('ep'), P(None, None), P('ep', None, None), P('ep', None, None), P('ep', None))
    out_specs = (P(), P('ep', None), P('ep', None, None), P('ep', None, None), P(None, None))
    return jax.shard_map(local_step, mesh=mesh, in_specs=in_specs, out_specs=out_specs, check_vma=False)
```

time: 445 us -> 240 us (0.54)
  Pallas kernels: 0 us -> 232 us
  blocking collectives: 167 us -> 0 us
  waiting for transfers between devices: 92.8 us -> 0.01 us
  matrix products: 88.5 us -> 0 us
  local copies, waits for them, and re-layouts: 43.1 us -> 3.05 us
  other arithmetic: 23.9 us -> 0 us
  between operations: 16.9 us -> 0.66 us
  starting transfers between devices: 11.5 us -> 3.48 us
    pallas_call x0 -> x6, Pallas kernels: none -> 232 us  [the longest x1 120 us: local_step(): pl.pallas_call(functools.partial(expert_kernel, groups, capacity, scale),...]
    all_to_all x3 -> x1, waiting for transfers between devices: 92.8 us -> 0.01 us  [local_step(): lax.all_to_all(u_rows, 'ep', 0, 0, tiled=True).reshape(slots, hidden)]
    dot_general x9 -> x0, matrix products: 88.5 us -> none  [the longest x1 14.2 us: local_step(): jnp.einsum('sekh,sekf->ehf', recv_x, grad_pre, preferred_element_type=jnp...]
    psum x1 -> x0, blocking collectives: 79.6 us -> none  [local_step(): lax.psum(jnp.concatenate([jnp.sum(router_prob, axis=0), y_part[None]]), '...]
    all_to_all x1 -> x0, blocking collectives: 53.1 us -> none  [local_step(): recv_x = lax.all_to_all(send_x, 'ep', 0, 0, tiled=True).reshape(recv_shape)]
    unnamed x1 -> x0, blocking collectives: 34.7 us -> none
    gather x4 -> x0, local copies, waits for them, and re-layouts: 32.7 us -> none  [the longest x1 10.7 us: local_step(): jnp.take(g_tok, src_safe, axis=0)]
    reduce_sum x7 -> x0, other arithmetic: 9.52 us -> none  [the longest x1 6.15 us: local_step(): d_gate = keep_f * grad_scale * jnp.sum(probe_f * z_tok, axis=1)]
  transfers between devices with their start and end apart: 4 -> 1, of which waited for: 2 -> 0; matrix products, arithmetic and copies ran while one was open for 17% -> 1% of each run, Pallas kernels for 0% -> 39%
where the time goes in v1:
time: 240 us
  Pallas kernels  232 us (97%)
  starting transfers between devices  3.48 us (1%)
  local copies, waits for them, and re-layouts  3.05 us (1%)
    pallas_call x1, Pallas kernels, local_step(): pl.pallas_call(functools.partial(expert_kernel, groups, capacity, scale),...  120 us
    pallas_call x1, Pallas kernels, local_step(): pl.pallas_call(functools.partial(router_kernel, groups, pair, scale, all_...  73.1 us
    pallas_call x1, Pallas kernels, local_step(): pl.pallas_call(weight_kernel, grid=(local,), out_shape=[sds((local, hidde...  20.5 us
    pallas_call x1, Pallas kernels, local_step(): pl.pallas_call(pack_kernel, grid=(steps,), out_shape=[sds((slots, hidden)...  8.31 us
    pallas_call x1, Pallas kernels, local_step(): pl.pallas_call(functools.partial(token_kernel, scale), grid=(steps,), out...  6.72 us
  transfers between devices with their start and end apart: 1, of which 0 were waited for; matrix products, arithmetic and copies ran while one was open for 1% of the time, Pallas kernels for 39%

profile of v1, /device:TPU:0, one launch (start us, length us, event | category | flops | bytes accessed | tf_op | source)
XLA Modules:
  0.0 239.6 jit_solution(7158403128725800605)
XLA Ops:
  0.6 3.6 %route.1 = (f32[64,512]{1,0:T(8,128)}, s32[8,512]{1,0:T(8,128)}, f32[64,128]{1,0:T(8,128)}) custom-call(s32[1,512]{1,0:T(1,128)} %bitcast.17, bf16[512,2048]{1,0:T(8,128)(2,1)} %x_ref.5, bf16[64,2048]{1,0:T(8,128)(2,1)} %bitcast.15), custom_call_target="tpu_custom_call" | custom-call | tf_op jit(solution)/shard_map/route/pallas_call | solution.py:306
  4.2 8.3 %pack.1 = (bf16[1024,2048]{1,0:T(8,128)(2,1)}, bf16[1024,2048]{1,0:T(8,128)(2,1)}) custom-call(s32[8,512]{1,0:T(8,128)} %get-tuple-element.22.meta_ref, bf16[512,2048]{1,0:T(8,128)(2,1)} %x_ref.5, bf16[512,2048]{1,0:T(8,128)(2,1)} %r_ref.5), custom_call_target="tpu_custom_call" | custom-call | tf_op jit(solution)/shard_map/pack/pallas_call | solution.py:314
  12.5 120.2 %experts.1 = (bf16[4,16,16,2048]{3,2,1,0:T(8,128)(2,1)}, bf16[4,256,1408]{2,1,0:T(8,128)(2,1)}, bf16[4,256,2048]{2,1,0:T(8,128)(2,1)}, bf16[4,256,1408]{2,1,0:T(...) custom-call(f32[64,128]{1,0:T(8,128)} %get-tuple-element.24.msg_ref, ...), custom_call_target="tpu_custom_call" | custom-call | tf_op jit(solution)/shard_map/experts/pallas_call | solution.py:324
  132.7 3.5 %all-to-all-start = ((bf16[16,4,16,2048]{3,2,1,0:T(8,128)(2,1)}), bf16[16,4,16,2048]{3,2,1,0:T(8,128)(2,1)}, u32[]{:S(2)}, u32[]{:S(2)}) async-start(bf16[16,4,16,2048]{3,2,1,0:T(8,128)(2,1)} %get-tuple-element.30), calls=%async_computation | async-start | bytes 8388608 | tf_op jit(solution)/shard_map/all_to_all | solution.py:340
  136.2 73.1 %router.1 = (bf16[64,512]{1,0:T(8,128)(2,1)}, f32[16,64,128]{2,1,0:T(8,128)}, f32[8,128]{1,0:T(8,128)}) custom-call(s32[1,512]{1,0:T(1,128)} %bitcast.18, s32[8,512]{1,0:T(8,128)} %get-tuple-element.22.meta_ref, f32[64,512]{1,0:T(8,128)} %get-tuple-element.23.p_ref, f32[16,64,128]{2,1,0:T(8,128)} %get-tuple-element.27.stat_ref, ...), custom_call_target="tpu_custom_call" | custom-call | flops 30000001024 | bytes 8000000 | tf_op jit(solution)/shard_map/router/pallas_call | solution.py:350
  209.3 1.2 slice.3
  210.5 1.9 copy_bitcast_fusion
  212.4 20.5 %weights.1 = (bf16[4,2048,1408]{2,1,0:T(8,128)(2,1)}, bf16[4,1408,2048]{2,1,0:T(8,128)(2,1)}) custom-call(bf16[4,256,2048]{2,1,0:T(8,128)(2,1)} %bitcast.19, bf16[4,256,1408]{2,1,0:T(8,128)(2,1)} %get-tuple-element.33.h_ref, bf16[4,256,2048]{2,1,0:T(8,128)(2,1)} %get-tuple-element.34.g_ref, bf16[4,256,1408]{2,1,0:T(8,128)(2,1)} %get-tuple-element.35.q_ref), custom_call_target="tpu_custom_call" | custom-call | flops 11811160064 | bytes 50000000 | tf_op jit(solution)/shard_map/weights/pallas_call | solution.py:342
  232.8 0.0 all-to-all-done
  232.8 6.7 %tokens.1 = bf16[512,2048]{1,0:T(8,128)(2,1)} custom-call(s32[8,512]{1,0:T(8,128)} %get-tuple-element.22.meta_ref, bf16[1024,2048]{1,0:T(8,128)(2,1)} %bitcast.5.u_ref, bf16[512,2048]{1,0:T(8,128)(2,1)} %r_ref.5, bf16[64,512]{1,0:T(8,128)(2,1)} %get-tuple-element.31.l_ref, bf16[64,2048]{1,0:T(8,128)(2,1)} %bitcast.16), custom_call_target="tpu_custom_call" | custom-call | tf_op jit(solution)/shard_map/tokens/pallas_call | solution.py:363
Async XLA Ops:
  132.7 100.1 %all-to-all-start = ((bf16[16,4,16,2048]{3,2,1,0:T(8,128)(2,1)}), bf16[16,4,16,2048]{3,2,1,0:T(8,128)(2,1)}, u32[]{:S(2)}, u32[]{:S(2)}) async-start(bf16[16,4,16,2048]{3,2,1,0:T(8,128)(2,1)} %get-tuple-element.30), calls=%async_computation | async-start | bytes 8388608 | tf_op jit(solution)/shard_map/all_to_all | solution.py:340

commit v2 on v0

v2 whole, which is shorter than its diff:
```python
import functools

import jax
import jax.numpy as jnp
from jax import lax
from jax.experimental import pallas as pl
from jax.experimental.pallas import tpu as pltpu
from jax.sharding import PartitionSpec as P

AUX_WEIGHT = 0.01
LANES = 128
MESH = pl.DeviceIdType.MESH
F32 = jnp.float32
BF16 = jnp.bfloat16
ORDER = (8, 4, 2, 12, 10, 6, 14, 9, 5, 3, 13, 11, 7, 15, 1)
VMEM = pl.BlockSpec(memory_space=pltpu.VMEM)
HBM = pl.BlockSpec(memory_space=pl.ANY)
HI = lax.Precision.HIGHEST
NT = (((1,), (1,)), ((), ()))
TN = (((0,), (0,)), ((), ()))


def dot(a, b, dims=(((1,), (0,)), ((), ())), **kw):
    return lax.dot_general(a, b, dims, preferred_element_type=F32, **kw)


def iota(shape, axis):
    return lax.broadcasted_iota(jnp.int32, shape, axis)


def greet(me, groups):
    barrier = pltpu.get_barrier_semaphore()
    for k in range(1, groups):
        pl.semaphore_signal(barrier, inc=1, device_id=(me ^ k,), device_id_type=MESH)
    pl.semaphore_wait(barrier, groups - 1)


def layer_kernel(groups, capacity, scale, all_tokens, idx_ref, x_ref, r_ref, wr_ref, w1_ref, w2_ref,
                 x_out, h_out, g_out, q_out, u_out, u_back, l_out, dwr_out, loss_out, meta_out,
                 xsend, rsend, xbuf, rbuf, usend, msg, mbuf, zsend, zbuf, p_buf, part, got, red, dwr, lsend, lgot,
                 send, recv, msend, mrecv, zss, zrs, uss, urs, s1, r1, s2, r2, s3, r3, own, uown, xsem):
    step = pl.program_id(0)
    last = pl.num_programs(0) - 1
    me = lax.axis_index('ep')
    local, _, pair, hidden = xbuf.shape
    experts, tok = p_buf.shape
    rows = groups * pair
    half = pair // 2
    early = usend.shape[0]

    def remote(src, dst, ssem, rsem, k):
        return pltpu.make_async_remote_copy(src_ref=src, dst_ref=dst, send_sem=ssem, recv_sem=rsem,
                                            device_id=(me ^ k,), device_id_type=MESH)

    def msg_copy(k, dev):
        return remote(msg, mbuf.at[dev], msend.at[k], mrecv.at[dev], k)

    def row_copy(t, c, k, dev):
        src, buf = ((xsend, xbuf), (rsend, rbuf))[t]
        return remote(src.at[c, me ^ k], buf.at[c, dev], send.at[t, c, k], recv.at[t, c, dev], k)

    def own_copy(t, c):
        src, buf = ((xsend, xbuf), (rsend, rbuf))[t]
        return pltpu.make_async_copy(src.at[c, me], buf.at[c, me], own.at[t, c])

    def z_copy(k, dev):
        return remote(zsend.at[me ^ k], zbuf.at[dev], zss.at[k], zrs.at[dev], k)

    def u_copy(c, s, k, dev):
        return remote(usend.at[c, me ^ k, pl.ds(s * half, half)], u_back.at[dev, c, pl.ds(s * half, half)],
                      uss.at[c, s, k], urs.at[c, s, dev], k)

    def u_own(c):
        return pltpu.make_async_copy(usend.at[c, me], u_back.at[me, c], uown.at[c])

    def rs_copy(k, dev):
        return remote(part.at[me ^ k], got.at[dev], s1.at[k], r1.at[dev], k)

    def ls_copy(k, dev):
        return remote(lsend, lgot.at[dev], s3.at[k], r3.at[dev], k)

    def ag_copy(k, dev):
        return remote(red, dwr.at[dev], s2.at[k], r2.at[dev], k)

    @pl.when(step == 0)
    def _():
        greet(me, groups)
        idx = idx_ref[...]
        onehot = (iota((experts, tok), 0) == idx).astype(F32)
        upper = (iota((tok, tok), 0) < iota((tok, tok), 1)).astype(BF16)
        before = dot(onehot.astype(BF16), upper)
        rank = jnp.sum(onehot * before, axis=0, keepdims=True).astype(jnp.int32)
        slot_of = idx * pair + rank
        meta_out[0:1, :] = slot_of
        meta_out[1:2, :] = rank
        meta_out[2:, :] = jnp.zeros((meta_out.shape[0] - 2, tok), jnp.int32)

        def chunk(c, _):
            row = iota((rows, tok), 0)
            want = (row // pair) * (local * pair) + c * pair + lax.rem(row, pair)
            pick = (want == slot_of).astype(BF16)
            xsend[c] = dot(pick, x_ref[...]).astype(BF16).reshape(groups, pair, hidden)
            rsend[c] = dot(pick, r_ref[...]).astype(BF16).reshape(groups, pair, hidden)
            for t in range(2):
                own_copy(t, c).start()
                for k in ORDER:
                    row_copy(t, c, k, me).start()
            return 0

        chunk(0, 0)
        logits = dot(wr_ref[...], x_ref[...], NT)
        ex = jnp.exp(logits - jnp.max(logits, axis=0, keepdims=True))
        p = ex / jnp.sum(ex, axis=0, keepdims=True)
        p_buf[...] = p
        gate = jnp.sum(onehot * p, axis=0, keepdims=True)
        rank_hot = (iota((LANES, tok), 0) == rank).astype(F32)
        table = dot(onehot * gate, rank_hot, NT, precision=HI)
        lane = iota((experts, LANES), 1)
        msg[...] = jnp.where(lane == pair, jnp.sum(onehot, axis=1, keepdims=True),
                             jnp.where(lane == pair + 1, jnp.sum(p, axis=1, keepdims=True), table))
        for k in ORDER:
            msg_copy(k, me).start()
        lax.fori_loop(1, local, chunk, 0)
        mbuf[me] = msg[...]
        for k in ORDER:
            msg_copy(k, me ^ k).wait_recv()

    @pl.when(step == 1)
    def _():
        prod = x_ref[...].astype(F32) * r_ref[...].astype(F32)
        xr = jnp.sum(jnp.sum(prod, axis=0, keepdims=True), axis=1, keepdims=True)
        lsend[...] = jnp.broadcast_to(xr, lsend.shape)

    gates, offs = [], []
    off = jnp.zeros((1, LANES), F32)
    for s in range(groups):
        row = mbuf[s, pl.ds(me * local + step, 1), :]
        gates.append(jnp.broadcast_to(row, (pair, LANES)))
        offs.append(jnp.broadcast_to(off, (pair, LANES)))
        off = off + row
    slot = lax.rem(iota((rows, LANES), 0), pair)
    lane = iota((rows, LANES), 1)
    gate = jnp.sum(jnp.where(lane == slot, jnp.concatenate(gates, axis=0), 0.0), axis=1, keepdims=True)
    ahead = jnp.sum(jnp.where(lane == pair, jnp.concatenate(offs, axis=0), 0.0), axis=1, keepdims=True)
    place = ahead + lax.rem(iota((rows, 1), 0), pair).astype(F32)
    keep = (place < float(capacity)).astype(F32)

    own_copy(0, step).wait()
    for k in ORDER:
        row_copy(0, step, k, me ^ k).wait_recv()
    x_save = pltpu.make_async_copy(xbuf.at[step], x_out.at[step], xsem)
    x_save.start()
    h = jnp.maximum(dot(xbuf[step].reshape(rows, hidden), w1_ref[0]), 0.0).astype(BF16)
    h_out[0] = h
    z = dot(h, w2_ref[0]).astype(BF16).astype(F32)
    own_copy(1, step).wait()
    for k in ORDER:
        row_copy(1, step, k, me ^ k).wait_recv()
    r = rbuf[step].reshape(rows, hidden).astype(F32)
    rz = keep * jnp.sum(r * z, axis=1, keepdims=True)
    rz_rows = jnp.sum(jnp.where(lane == slot, rz, 0.0).reshape(groups, pair, LANES), axis=1)
    for s in range(groups):
        zsend[s, pl.ds(step, 1), :] = rz_rows[s:s + 1, :]
    g = ((keep * gate * scale) * r).astype(BF16)
    g_out[0] = g

    @pl.when(step == last)
    def _():
        for k in ORDER:
            z_copy(k, me).start()
        for k in ORDER:
            u_copy(0, 0, k, me).start()

    dh = dot(g, w2_ref[0], NT)
    q = jnp.where(h_out[0].astype(F32) > 0.0, dh, 0.0).astype(BF16)
    q_out[0] = q
    u = dot(q, w1_ref[0], NT).astype(BF16)

    @pl.when(step < early)
    def _():
        usend[step] = u.reshape(groups, pair, hidden)

    @pl.when(step >= early)
    def _():
        u_out[...] = u.reshape(groups, 1, pair, hidden)

    x_save.wait()

    @pl.when(step == last)
    def _():
        zbuf[me] = zsend[me]
        for k in ORDER:
            z_copy(k, me ^ k).wait_recv()
        onehot = (iota((experts, tok), 0) == idx_ref[...]).astype(F32)
        rank_hot = iota((LANES, tok), 0) == meta_out[1:2, :]
        p = p_buf[...]
        gate = jnp.sum(onehot * p, axis=0, keepdims=True)
        table = jnp.concatenate([zbuf[d, 0:local, :] for d in range(groups)], axis=0)
        rz_all = dot(table, onehot, TN, precision=HI)
        rz = jnp.sum(jnp.where(rank_hot, rz_all, 0.0), axis=0, keepdims=True)
        stat = jnp.zeros((experts, LANES), F32)
        for d in range(groups):
            stat = stat + mbuf[d]
        lane = iota((experts, LANES), 1)
        frac = jnp.sum(jnp.where(lane == pair, stat, 0.0), axis=1, keepdims=True) / float(all_tokens)
        p_mean = jnp.sum(jnp.where(lane == pair + 1, stat, 0.0), axis=1, keepdims=True) / float(all_tokens)
        aux = AUX_WEIGHT * experts * jnp.sum(frac * p_mean, axis=0, keepdims=True)
        coef = (AUX_WEIGHT * experts / all_tokens) * frac
        d_task = ((scale * rz) * gate) * (onehot - p)
        d_aux = p * (coef - jnp.sum(p * coef, axis=0, keepdims=True))
        l = (d_task + d_aux).astype(BF16)
        l_out[...] = l
        for d in range(groups):
            part[d] = dot(l, x_ref[:, d * LANES:(d + 1) * LANES])
        lsend[...] = lsend[...] + jnp.sum(gate * rz, axis=1, keepdims=True)
        for k in ORDER:
            rs_copy(k, me).start()
        for k in ORDER:
            ls_copy(k, me).start()
        for k in ORDER:
            u_copy(0, 1, k, me).start()
        for c in range(early):
            u_own(c).start()
        for k in ORDER:
            rs_copy(k, me ^ k).wait_recv()
        got[me] = part[me]
        total = got[0]
        for d in range(1, groups):
            total = total + got[d]
        red[...] = total
        for k in ORDER:
            ag_copy(k, me).start()
        for c in range(1, early):
            for s in range(2):
                for k in ORDER:
                    u_copy(c, s, k, me).start()
        for k in ORDER:
            ls_copy(k, me ^ k).wait_recv()
        lgot[me] = lsend[...]
        y = lgot[0]
        for d in range(1, groups):
            y = y + lgot[d]
        loss_out[...] = y * scale + aux
        dwr[me] = total
        for k in ORDER:
            ag_copy(k, me ^ k).wait_recv()
        dwr_out[...] = dwr[...]
        for c in range(early):
            for s in range(2):
                for k in ORDER:
                    u_copy(c, s, k, me ^ k).wait_recv()
            u_own(c).wait()
        for k in ORDER:
            msg_copy(k, me).wait_send()
            z_copy(k, me).wait_send()
            rs_copy(k, me).wait_send()
            ls_copy(k, me).wait_send()
            ag_copy(k, me).wait_send()

        def sent(c, _):
            for t in range(2):
                for k in ORDER:
                    row_copy(t, c, k, me).wait_send()
            return 0
        lax.fori_loop(0, local, sent, 0)
        for c in range(early):
            for s in range(2):
                for k in ORDER:
                    u_copy(c, s, k, me).wait_send()


def weight_kernel(x_ref, h_ref, g_ref, q_ref, d1_ref, d2_ref):
    d1_ref[0] = dot(x_ref[0], q_ref[0], TN).astype(BF16)
    d2_ref[0] = dot(h_ref[0], g_ref[0], TN).astype(BF16)


def picked(meta_ref, first, pair, early, local, count, tok):
    row = iota((count, tok), 0)
    span = early * pair
    want = (row // span) * (local * pair) + first * pair + lax.rem(row, span)
    return (want == meta_ref[0:1, :]).astype(BF16)


def token_first_kernel(scale, pair, early, local, meta_ref, u_ref, r_ref, l_ref, wr_ref, o_ref):
    pick = picked(meta_ref, 0, pair, early, local, u_ref.shape[0], r_ref.shape[0])
    u = dot(pick, u_ref[...], TN)
    dx = dot(l_ref[...], wr_ref[...], TN)
    o_ref[...] = scale * r_ref[...].astype(F32) + u + dx


def token_last_kernel(pair, early, local, meta_ref, u_ref, a_ref, o_ref):
    pick = picked(meta_ref, early, pair, local - early, local, u_ref.shape[0], a_ref.shape[0])
    o_ref[...] = (a_ref[...] + dot(pick, u_ref[...], TN)).astype(BF16)


def params(**kw):
    return pltpu.CompilerParams(vmem_limit_bytes=62 * 2 ** 20, **kw)


def solution(mesh):
    groups = mesh.shape['ep']

    def local_step(tokens, expert_idx, w_router, w_in, w_out, loss_probe):
        tok, hidden = tokens.shape
        local, _, ffn = w_in.shape
        experts = w_router.shape[1]
        all_tokens = tok * groups
        capacity = (5 * all_tokens + 4 * experts - 1) // (4 * experts)
        pair = 2 * tok // experts
        slots = experts * pair
        rows = groups * pair
        scale = 1.0 / (all_tokens * hidden)
        sds = jax.ShapeDtypeStruct
        idx = expert_idx.reshape(1, tok)
        wr_t = w_router.T

        steps = 4
        early = 2
        full = lambda shape: pl.BlockSpec(shape, lambda i: (0,) * len(shape))
        per = lambda shape: pl.BlockSpec((1,) + shape, lambda i: (i,) + (0,) * len(shape))
        vm = lambda *shape: pltpu.VMEM(shape, BF16)
        vf = lambda *shape: pltpu.VMEM(shape, F32)
        dma = lambda *shape: pltpu.SemaphoreType.DMA(shape)
        x_buf, h_buf, g_buf, q_buf, u_late, u_early, l_t, d_wr, loss, meta = pl.pallas_call(
            functools.partial(layer_kernel, groups, capacity, scale, all_tokens), grid=(local,),
            out_shape=[sds((local, groups, pair, hidden), BF16), sds((local, rows, ffn), BF16), sds((local, rows, hidden), BF16),
                       sds((local, rows, ffn), BF16), sds((groups, local - early, pair, hidden), BF16),
                       sds((groups, early, pair, hidden), BF16), sds((experts, tok), BF16),
                       sds((groups, experts, LANES), F32), sds((8, LANES), F32), sds((8, tok), jnp.int32)],
            in_specs=[VMEM, VMEM, VMEM, VMEM, per((hidden, ffn)), per((ffn, hidden))],
            out_specs=[HBM, per((rows, ffn)), per((rows, hidden)), per((rows, ffn)),
                       pl.BlockSpec((groups, 1, pair, hidden), lambda i: (0, jnp.maximum(i - early, 0), 0, 0)),
                       HBM, VMEM, VMEM, VMEM, VMEM],
            scratch_shapes=[vm(local, groups, pair, hidden)] * 4
            + [vm(early, groups, pair, hidden), vf(experts, LANES), vf(groups, experts, LANES), vf(groups, 8, LANES),
               vf(groups, 8, LANES), vf(experts, tok), vf(groups, experts, LANES), vf(groups, experts, LANES),
               vf(experts, LANES), vf(groups, experts, LANES), vf(8, LANES), vf(groups, 8, LANES),
               dma(2, local, groups), dma(2, local, groups)] + [dma(groups)] * 4
            + [dma(early, 2, groups)] * 2 + [dma(groups)] * 6 + [dma(2, local), dma(early), pltpu.SemaphoreType.DMA],
            name='layer',
            compiler_params=params(collective_id=0, has_side_effects=True))(
                idx, tokens, loss_probe, wr_t, w_in, w_out)

        u_late = lax.all_to_all(u_late, 'ep', 0, 0, tiled=True).reshape(groups * (local - early) * pair, hidden)
        u_early = u_early.reshape(groups * early * pair, hidden)

        d_w_in, d_w_out = pl.pallas_call(
            weight_kernel, grid=(local,),
            out_shape=[sds((local, hidden, ffn), BF16), sds((local, ffn, hidden), BF16)],
            in_specs=[per((rows, hidden)), per((rows, ffn)), per((rows, hidden)), per((rows, ffn))],
            out_specs=[per((hidden, ffn)), per((ffn, hidden))], name='weights',
            cost_estimate=pl.CostEstimate(flops=4 * local * rows * hidden * ffn, bytes_accessed=50_000_000, transcendentals=0),
            compiler_params=params())(x_buf.reshape(local, rows, hidden), h_buf, g_buf, q_buf)

        cols = hidden // steps
        col = lambda r: pl.BlockSpec((r, cols), lambda i: (0, i))
        acc = pl.pallas_call(
            functools.partial(token_first_kernel, scale, pair, early, local), grid=(steps,),
            out_shape=sds((tok, hidden), F32),
            in_specs=[full((8, tok)), col(u_early.shape[0]), col(tok), full((experts, tok)), col(experts)],
            out_specs=col(tok), name='first',
            cost_estimate=pl.CostEstimate(flops=4_000_000_000, bytes_accessed=8_000_000, transcendentals=0),
            compiler_params=params())(meta, u_early, loss_probe, l_t, wr_t)
        d_tokens = pl.pallas_call(
            functools.partial(token_last_kernel, pair, early, local), grid=(steps,),
            out_shape=sds((tok, hidden), BF16),
            in_specs=[full((8, tok)), col(u_late.shape[0]), col(tok)],
            out_specs=col(tok), name='last',
            compiler_params=params())(meta, u_late, acc)

        d_w_router = d_wr.transpose(0, 2, 1).reshape(hidden, experts)
        return loss[0, 0], d_tokens, d_w_in, d_w_out, d_w_router

    in_specs = (P('ep', None), P('ep'), P(None, None), P('ep', None, None), P('ep', None, None), P('ep', None))
    out_specs = (P(), P('ep', None), P('ep', None, None), P('ep', None, None), P(None, None))
    return jax.shard_map(local_step, mesh=mesh, in_specs=in_specs, out_specs=out_specs, check_vma=False)
```

time: 445 us -> 196 us (0.44)
  Pallas kernels: 0 us -> 190 us
  blocking collectives: 167 us -> 0 us
  waiting for transfers between devices: 92.8 us -> 0.01 us
  matrix products: 88.5 us -> 0 us
  local copies, waits for them, and re-layouts: 43.1 us -> 2.02 us
  other arithmetic: 23.9 us -> 0 us
  between operations: 16.9 us -> 0.65 us
  starting transfers between devices: 11.5 us -> 3.2 us
    pallas_call x0 -> x4, Pallas kernels: none -> 190 us  [the longest x1 158 us: local_step(): pl.pallas_call(functools.partial(layer_kernel, groups, capacity, scale, a...]
    all_to_all x3 -> x1, waiting for transfers between devices: 92.8 us -> 0.01 us  [local_step(): lax.all_to_all(u_late, 'ep', 0, 0, tiled=True)]
    dot_general x9 -> x0, matrix products: 88.5 us -> none  [the longest x1 14.2 us: local_step(): jnp.einsum('sekh,sekf->ehf', recv_x, grad_pre, preferred_element_type=jnp...]
    psum x1 -> x0, blocking collectives: 79.6 us -> none  [local_step(): lax.psum(jnp.concatenate([jnp.sum(router_prob, axis=0), y_part[None]]), '...]
    all_to_all x1 -> x0, blocking collectives: 53.1 us -> none  [local_step(): recv_x = lax.all_to_all(send_x, 'ep', 0, 0, tiled=True).reshape(recv_shape)]
    unnamed x1 -> x0, blocking collectives: 34.7 us -> none
    gather x4 -> x0, local copies, waits for them, and re-layouts: 32.7 us -> none  [the longest x1 10.7 us: local_step(): jnp.take(g_tok, src_safe, axis=0)]
    reduce_sum x7 -> x0, other arithmetic: 9.52 us -> none  [the longest x1 6.15 us: local_step(): d_gate = keep_f * grad_scale * jnp.sum(probe_f * z_tok, axis=1)]
  transfers between devices with their start and end apart: 4 -> 1, of which waited for: 2 -> 0; matrix products, arithmetic and copies ran while one was open for 17% -> 1% of each run, Pallas kernels for 0% -> 14%
where the time goes in v2:
time: 196 us
  Pallas kernels  190 us (97%)
  starting transfers between devices  3.2 us (2%)
  local copies, waits for them, and re-layouts  2.02 us (1%)
    pallas_call x1, Pallas kernels, local_step(): pl.pallas_call(functools.partial(layer_kernel, groups, capacity, scale, a...  158 us
    pallas_call x1, Pallas kernels, local_step(): pl.pallas_call(weight_kernel, grid=(local,), out_shape=[sds((local, hidde...  20.5 us
    pallas_call x1, Pallas kernels, local_step(): pl.pallas_call(functools.partial(token_first_kernel, scale, pair, early,...  6.12 us
    pallas_call x1, Pallas kernels, local_step(): pl.pallas_call(functools.partial(token_last_kernel, pair, early, local),...  5.55 us
  transfers between devices with their start and end apart: 1, of which 0 were waited for; matrix products, arithmetic and copies ran while one was open for 1% of the time, Pallas kernels for 14%

profile of v2, /device:TPU:0, one launch (start us, length us, event | category | flops | bytes accessed | tf_op | source)
XLA Modules:
  0.0 195.6 jit_solution(13769292557878110979)
XLA Ops:
  0.6 157.6 %layer.1 = (bf16[4,16,16,2048]{3,2,1,0:T(8,128)(2,1)}, bf16[4,256,1408]{2,1,0:T(8,128)(2,1)}, bf16[4,256,2048]{2,1,0:T(8,128)(2,1)}, bf16[4,256,1408]{2,1,0:T(8,...) custom-call(s32[1,512]{1,0:T(1,128)} %bitcast.14, ...), custom_call_target="tpu_custom_call" | custom-call | tf_op jit(solution)/shard_map/layer/pallas_call | solution.py:324
  158.3 3.2 %all-to-all-start = ((bf16[16,2,16,2048]{3,2,1,0:T(8,128)(2,1)}), bf16[16,2,16,2048]{3,2,1,0:T(8,128)(2,1)}, u32[]{:S(2)}, u32[]{:S(2)}) async-start(bf16[16,2,16,2048]{3,2,1,0:T(8,128)(2,1)} %get-tuple-element.19), calls=%async_computation | async-start | bytes 4194304 | tf_op jit(solution)/shard_map/all_to_all | solution.py:344
  161.5 1.2 slice.3
  162.7 0.0 copy-start
  162.7 6.1 %first.1.a_ref = f32[512,2048]{1,0:T(8,128)} custom-call(s32[8,512]{1,0:T(8,128)} %get-tuple-element.18.meta_ref, bf16[512,2048]{1,0:T(8,128)(2,1)} %bitcast.16, bf16[512,2048]{1,0:T(8,128)(2,1)} %r_ref.3, bf16[64,512]{1,0:T(8,128)(2,1)} %get-tuple-element.21.l_ref, bf16[64,2048]{1,0:T(8,128)(2,1)} %bitcast.13), custom_call_target="tpu_custom_call" | custom-call | flops 4000000000 | bytes 8000000 | tf_op jit(solution)/shard_map/first/pallas_call | solution.py:357
  168.8 0.0 copy-done
  168.8 0.8 copy_bitcast_fusion
  169.6 20.5 %weights.1 = (bf16[4,2048,1408]{2,1,0:T(8,128)(2,1)}, bf16[4,1408,2048]{2,1,0:T(8,128)(2,1)}) custom-call(bf16[4,256,2048]{2,1,0:T(8,128)(2,1)} %bitcast.15, bf16[4,256,1408]{2,1,0:T(8,128)(2,1)} %get-tuple-element.23.h_ref, bf16[4,256,2048]{2,1,0:T(8,128)(2,1)} %get-tuple-element.24.g_ref, bf16[4,256,1408]{2,1,0:T(8,128)(2,1)} %get-tuple-element.25.q_ref), custom_call_target="tpu_custom_call" | custom-call | flops 11811160064 | bytes 50000000 | tf_op jit(solution)/shard_map/weights/pallas_call | solution.py:347
  190.1 0.0 all-to-all-done
  190.1 5.6 %last.1 = bf16[512,2048]{1,0:T(8,128)(2,1)} custom-call(s32[8,512]{1,0:T(8,128)} %get-tuple-element.18.meta_ref, bf16[512,2048]{1,0:T(8,128)(2,1)} %bitcast.3.u_ref, f32[512,2048]{1,0:T(8,128)} %first.1.a_ref), custom_call_target="tpu_custom_call" | custom-call | tf_op jit(solution)/shard_map/last/pallas_call | solution.py:364
Async XLA Ops:
  158.3 31.8 %all-to-all-start = ((bf16[16,2,16,2048]{3,2,1,0:T(8,128)(2,1)}), bf16[16,2,16,2048]{3,2,1,0:T(8,128)(2,1)}, u32[]{:S(2)}, u32[]{:S(2)}) async-start(bf16[16,2,16,2048]{3,2,1,0:T(8,128)(2,1)} %get-tuple-element.19), calls=%async_computation | async-start | bytes 4194304 | tf_op jit(solution)/shard_map/all_to_all | solution.py:344
  162.7 6.1 %copy-start = (f32[16,64,128]{2,1,0:T(8,128)S(1)}, f32[16,64,128]{2,1,0:T(8,128)}, u32[]{:S(2)}) copy-start(f32[16,64,128]{2,1,0:T(8,128)} %get-tuple-element.28) | copy-start | bytes 1572868

commit v3 on v2

--- a/solution.py
+++ b/solution.py
@@ -35,10 +35,10 @@
     pl.semaphore_wait(barrier, groups - 1)
 
 
-def layer_kernel(groups, capacity, scale, all_tokens, idx_ref, x_ref, r_ref, wr_ref, w1_ref, w2_ref,
+def layer_kernel(groups, capacity, scale, all_tokens, idx_ref, x_ref, r_ref, wr_ref, w1_hbm, w2_hbm,
                  x_out, h_out, g_out, q_out, u_out, u_back, l_out, dwr_out, loss_out, meta_out,
-                 xsend, rsend, xbuf, rbuf, usend, msg, mbuf, zsend, zbuf, p_buf, part, got, red, dwr, lsend, lgot,
-                 send, recv, msend, mrecv, zss, zrs, uss, urs, s1, r1, s2, r2, s3, r3, own, uown, xsem):
+                 xsend, rsend, xbuf, rbuf, usend, msg, mbuf, zsend, zbuf, p_buf, part, sib, got, red, dwr, lsend, lgot, w1_buf, w2_buf,
+                 send, recv, msend, mrecv, zss, zrs, uss, urs, s1, r1, s2, r2, s3, r3, cs, own, uown, xsem, wsem):
     step = pl.program_id(0)
     last = pl.num_programs(0) - 1
     me = lax.axis_index('ep')
@@ -47,13 +47,16 @@
     rows = groups * pair
     half = pair // 2
     early = usend.shape[0]
+    chips = groups // 2
+    chip, core = me // 2, lax.rem(me, 2)
+    far = tuple(k for k in ORDER if k % 2 == 0)
 
     def remote(src, dst, ssem, rsem, k):
         return pltpu.make_async_remote_copy(src_ref=src, dst_ref=dst, send_sem=ssem, recv_sem=rsem,
                                             device_id=(me ^ k,), device_id_type=MESH)
 
     def msg_copy(k, dev):
-        return remote(msg, mbuf.at[dev], msend.at[k], mrecv.at[dev], k)
+        return remote(msg.at[me ^ k], mbuf.at[dev], msend.at[k], mrecv.at[dev], k)
 
     def row_copy(t, c, k, dev):
         src, buf = ((xsend, xbuf), (rsend, rbuf))[t]
@@ -73,14 +76,24 @@
     def u_own(c):
         return pltpu.make_async_copy(usend.at[c, me], u_back.at[me, c], uown.at[c])
 
+    def pair_copy():
+        return remote(part.at[1 - core], sib, cs.at[0], cs.at[1], 1)
+
     def rs_copy(k, dev):
-        return remote(part.at[me ^ k], got.at[dev], s1.at[k], r1.at[dev], k)
+        return remote(part.at[core, (me ^ k) // 2], got.at[dev // 2], s1.at[k], r1.at[dev // 2], k)
 
     def ls_copy(k, dev):
         return remote(lsend, lgot.at[dev], s3.at[k], r3.at[dev], k)
 
     def ag_copy(k, dev):
-        return remote(red, dwr.at[dev], s2.at[k], r2.at[dev], k)
+        return remote(red, dwr.at[core, dev // 2], s2.at[k], r2.at[dev // 2], k)
+
+    def share_copy(b):
+        return remote(dwr.at[b], dwr.at[b], cs.at[2], cs.at[3], 1)
+
+    def w_copy(t, e):
+        src, buf = ((w1_hbm, w1_buf), (w2_hbm, w2_buf))[t]
+        return pltpu.make_async_copy(src.at[e], buf.at[lax.rem(e, 2)], wsem.at[t, lax.rem(e, 2)])
 
     @pl.when(step == 0)
     def _():
@@ -108,6 +121,8 @@
             return 0
 
         chunk(0, 0)
+        for t in range(2):
+            w_copy(t, 0).start()
         logits = dot(wr_ref[...], x_ref[...], NT)
         ex = jnp.exp(logits - jnp.max(logits, axis=0, keepdims=True))
         p = ex / jnp.sum(ex, axis=0, keepdims=True)
@@ -116,12 +131,20 @@
         rank_hot = (iota((LANES, tok), 0) == rank).astype(F32)
         table = dot(onehot * gate, rank_hot, NT, precision=HI)
         lane = iota((experts, LANES), 1)
-        msg[...] = jnp.where(lane == pair, jnp.sum(onehot, axis=1, keepdims=True),
-                             jnp.where(lane == pair + 1, jnp.sum(p, axis=1, keepdims=True), table))
+        ones = jnp.ones((8, tok), F32)
+        counts = dot(ones.astype(BF16), onehot.astype(BF16), NT)
+        p_sums = dot(ones, p, NT, precision=HI)
+        table = jnp.where(lane == pair, jnp.sum(onehot, axis=1, keepdims=True), table)
+        for d in range(groups):
+            msg[d, 0:local, :] = table[d * local:(d + 1) * local, :]
+            msg[d, local:local + 1, 0:experts] = counts[0:1, :]
+            msg[d, local + 1:local + 2, 0:experts] = p_sums[0:1, :]
+            msg[d, local:local + 2, experts:] = jnp.zeros((2, LANES - experts), F32)
+            msg[d, local + 2:, :] = jnp.zeros((msg.shape[1] - local - 2, LANES), F32)
         for k in ORDER:
             msg_copy(k, me).start()
         lax.fori_loop(1, local, chunk, 0)
-        mbuf[me] = msg[...]
+        mbuf[me] = msg[me]
         for k in ORDER:
             msg_copy(k, me ^ k).wait_recv()
 
@@ -134,7 +157,7 @@
     gates, offs = [], []
     off = jnp.zeros((1, LANES), F32)
     for s in range(groups):
-        row = mbuf[s, pl.ds(me * local + step, 1), :]
+        row = mbuf[s, pl.ds(step, 1), :]
         gates.append(jnp.broadcast_to(row, (pair, LANES)))
         offs.append(jnp.broadcast_to(off, (pair, LANES)))
         off = off + row
@@ -145,14 +168,23 @@
     place = ahead + lax.rem(iota((rows, 1), 0), pair).astype(F32)
     keep = (place < float(capacity)).astype(F32)
 
+    for t in range(2):
+        w_copy(t, step).wait()
+
+    @pl.when(step < last)
+    def _():
+        for t in range(2):
+            w_copy(t, step + 1).start()
+
+    slot_w = lax.rem(step, 2)
     own_copy(0, step).wait()
     for k in ORDER:
         row_copy(0, step, k, me ^ k).wait_recv()
     x_save = pltpu.make_async_copy(xbuf.at[step], x_out.at[step], xsem)
     x_save.start()
-    h = jnp.maximum(dot(xbuf[step].reshape(rows, hidden), w1_ref[0]), 0.0).astype(BF16)
+    h = jnp.maximum(dot(xbuf[step].reshape(rows, hidden), w1_buf[slot_w]), 0.0).astype(BF16)
     h_out[0] = h
-    z = dot(h, w2_ref[0]).astype(BF16).astype(F32)
+    z = dot(h, w2_buf[slot_w]).astype(BF16).astype(F32)
     own_copy(1, step).wait()
     for k in ORDER:
         row_copy(1, step, k, me ^ k).wait_recv()
@@ -171,10 +203,10 @@
         for k in ORDER:
             u_copy(0, 0, k, me).start()
 
-    dh = dot(g, w2_ref[0], NT)
+    dh = dot(g, w2_buf[slot_w], NT)
     q = jnp.where(h_out[0].astype(F32) > 0.0, dh, 0.0).astype(BF16)
     q_out[0] = q
-    u = dot(q, w1_ref[0], NT).astype(BF16)
+    u = dot(q, w1_buf[slot_w], NT).astype(BF16)
 
     @pl.when(step < early)
     def _():
@@ -198,42 +230,48 @@
         table = jnp.concatenate([zbuf[d, 0:local, :] for d in range(groups)], axis=0)
         rz_all = dot(table, onehot, TN, precision=HI)
         rz = jnp.sum(jnp.where(rank_hot, rz_all, 0.0), axis=0, keepdims=True)
-        stat = jnp.zeros((experts, LANES), F32)
-        for d in range(groups):
+        stat = mbuf[0]
+        for d in range(1, groups):
             stat = stat + mbuf[d]
-        lane = iota((experts, LANES), 1)
-        frac = jnp.sum(jnp.where(lane == pair, stat, 0.0), axis=1, keepdims=True) / float(all_tokens)
-        p_mean = jnp.sum(jnp.where(lane == pair + 1, stat, 0.0), axis=1, keepdims=True) / float(all_tokens)
+        diag = iota((experts, LANES), 0) == iota((experts, LANES), 1)
+        frac = jnp.sum(jnp.where(diag, stat[local:local + 1, :], 0.0), axis=1, keepdims=True) / float(all_tokens)
+        p_mean = jnp.sum(jnp.where(diag, stat[local + 1:local + 2, :], 0.0), axis=1, keepdims=True) / float(all_tokens)
         aux = AUX_WEIGHT * experts * jnp.sum(frac * p_mean, axis=0, keepdims=True)
         coef = (AUX_WEIGHT * experts / all_tokens) * frac
         d_task = ((scale * rz) * gate) * (onehot - p)
         d_aux = p * (coef - jnp.sum(p * coef, axis=0, keepdims=True))
         l = (d_task + d_aux).astype(BF16)
         l_out[...] = l
-        for d in range(groups):
-            part[d] = dot(l, x_ref[:, d * LANES:(d + 1) * LANES])
+        for d in range(chips):
+            both = dot(l, x_ref[:, 2 * d * LANES:2 * (d + 1) * LANES])
+            part[0, d] = both[:, :LANES]
+            part[1, d] = both[:, LANES:]
         lsend[...] = lsend[...] + jnp.sum(gate * rz, axis=1, keepdims=True)
-        for k in ORDER:
-            rs_copy(k, me).start()
+        pair_copy().start()
         for k in ORDER:
             ls_copy(k, me).start()
         for k in ORDER:
             u_copy(0, 1, k, me).start()
         for c in range(early):
             u_own(c).start()
-        for k in ORDER:
+        pair_copy().wait_recv()
+        for d in range(chips):
+            part[core, d] = part[core, d] + sib[d]
+        for k in far:
+            rs_copy(k, me).start()
+        for k in ORDER:
+            u_copy(1, 0, k, me).start()
+        for k in far:
             rs_copy(k, me ^ k).wait_recv()
-        got[me] = part[me]
+        got[chip] = part[core, chip]
         total = got[0]
-        for d in range(1, groups):
+        for d in range(1, chips):
             total = total + got[d]
         red[...] = total
-        for k in ORDER:
+        for k in far:
             ag_copy(k, me).start()
-        for c in range(1, early):
-            for s in range(2):
-                for k in ORDER:
-                    u_copy(c, s, k, me).start()
+        for k in ORDER:
+            u_copy(1, 1, k, me).start()
         for k in ORDER:
             ls_copy(k, me ^ k).wait_recv()
         lgot[me] = lsend[...]
@@ -241,10 +279,13 @@
         for d in range(1, groups):
             y = y + lgot[d]
         loss_out[...] = y * scale + aux
-        dwr[me] = total
-        for k in ORDER:
+        dwr[core, chip] = total
+        for k in far:
             ag_copy(k, me ^ k).wait_recv()
-        dwr_out[...] = dwr[...]
+        share_copy(core).start()
+        share_copy(1 - core).wait_recv()
+        for d in range(groups):
+            dwr_out[:, d * LANES:(d + 1) * LANES] = dwr[d % 2, d // 2]
         for c in range(early):
             for s in range(2):
                 for k in ORDER:
@@ -253,9 +294,12 @@
         for k in ORDER:
             msg_copy(k, me).wait_send()
             z_copy(k, me).wait_send()
+            ls_copy(k, me).wait_send()
+        for k in far:
             rs_copy(k, me).wait_send()
-            ls_copy(k, me).wait_send()
             ag_copy(k, me).wait_send()
+        pair_copy().wait_send()
+        share_copy(core).wait_send()
 
         def sent(c, _):
             for t in range(2):
@@ -274,23 +318,21 @@
     d2_ref[0] = dot(h_ref[0], g_ref[0], TN).astype(BF16)
 
 
-def picked(meta_ref, first, pair, early, local, count, tok):
-    row = iota((count, tok), 0)
-    span = early * pair
-    want = (row // span) * (local * pair) + first * pair + lax.rem(row, span)
-    return (want == meta_ref[0:1, :]).astype(BF16)
-
-
-def token_first_kernel(scale, pair, early, local, meta_ref, u_ref, r_ref, l_ref, wr_ref, o_ref):
-    pick = picked(meta_ref, 0, pair, early, local, u_ref.shape[0], r_ref.shape[0])
-    u = dot(pick, u_ref[...], TN)
+def pick_kernel(pair, early, local, meta_ref, first_ref, rest_ref):
+    tok = meta_ref.shape[1]
+    row = meta_ref[0:1, :].astype(F32)
+    slot = jnp.sum(jnp.where(iota((tok, tok), 0) == iota((tok, tok), 1), row, 0.0), axis=1, keepdims=True).astype(jnp.int32)
+    for first, count, o_ref in ((0, early, first_ref), (early, local - early, rest_ref)):
+        col = iota(o_ref.shape, 1)
+        span = count * pair
+        want = (col // span) * (local * pair) + first * pair + lax.rem(col, span)
+        o_ref[...] = (want == slot).astype(BF16)
+
+
+def token_kernel(scale, pick1_ref, pick2_ref, u1_ref, u2_ref, r_ref, l_ref, wr_ref, o_ref):
+    u = dot(pick1_ref[...], u1_ref[...]) + dot(pick2_ref[...], u2_ref[...])
     dx = dot(l_ref[...], wr_ref[...], TN)
-    o_ref[...] = scale * r_ref[...].astype(F32) + u + dx
-
-
-def token_last_kernel(pair, early, local, meta_ref, u_ref, a_ref, o_ref):
-    pick = picked(meta_ref, early, pair, local - early, local, u_ref.shape[0], a_ref.shape[0])
-    o_ref[...] = (a_ref[...] + dot(pick, u_ref[...], TN)).astype(BF16)
+    o_ref[...] = (scale * r_ref[...].astype(F32) + u + dx).astype(BF16)
 
 
 def params(**kw):
@@ -326,17 +368,18 @@
             out_shape=[sds((local, groups, pair, hidden), BF16), sds((local, rows, ffn), BF16), sds((local, rows, hidden), BF16),
                        sds((local, rows, ffn), BF16), sds((groups, local - early, pair, hidden), BF16),
                        sds((groups, early, pair, hidden), BF16), sds((experts, tok), BF16),
-                       sds((groups, experts, LANES), F32), sds((8, LANES), F32), sds((8, tok), jnp.int32)],
-            in_specs=[VMEM, VMEM, VMEM, VMEM, per((hidden, ffn)), per((ffn, hidden))],
+                       sds((experts, hidden), F32), sds((8, LANES), F32), sds((8, tok), jnp.int32)],
+            in_specs=[VMEM, VMEM, VMEM, VMEM, HBM, HBM],
             out_specs=[HBM, per((rows, ffn)), per((rows, hidden)), per((rows, ffn)),
                        pl.BlockSpec((groups, 1, pair, hidden), lambda i: (0, jnp.maximum(i - early, 0), 0, 0)),
                        HBM, VMEM, VMEM, VMEM, VMEM],
             scratch_shapes=[vm(local, groups, pair, hidden)] * 4
-            + [vm(early, groups, pair, hidden), vf(experts, LANES), vf(groups, experts, LANES), vf(groups, 8, LANES),
-               vf(groups, 8, LANES), vf(experts, tok), vf(groups, experts, LANES), vf(groups, experts, LANES),
-               vf(experts, LANES), vf(groups, experts, LANES), vf(8, LANES), vf(groups, 8, LANES),
-               dma(2, local, groups), dma(2, local, groups)] + [dma(groups)] * 4
-            + [dma(early, 2, groups)] * 2 + [dma(groups)] * 6 + [dma(2, local), dma(early), pltpu.SemaphoreType.DMA],
+            + [vm(early, groups, pair, hidden)] + [vf(groups, 8, LANES)] * 4
+            + [vf(experts, tok), vf(2, groups // 2, experts, LANES), vf(groups // 2, experts, LANES), vf(groups // 2, experts, LANES),
+               vf(experts, LANES), vf(2, groups // 2, experts, LANES), vf(8, LANES), vf(groups, 8, LANES),
+               vm(2, hidden, ffn), vm(2, ffn, hidden), dma(2, local, groups), dma(2, local, groups)] + [dma(groups)] * 4
+            + [dma(early, 2, groups)] * 2 + [dma(groups)] * 6
+            + [dma(4), dma(2, local), dma(early), pltpu.SemaphoreType.DMA, dma(2, 2)],
             name='layer',
             compiler_params=params(collective_id=0, has_side_effects=True))(
                 idx, tokens, loss_probe, wr_t, w_in, w_out)
@@ -354,21 +397,21 @@
 
         cols = hidden // steps
         col = lambda r: pl.BlockSpec((r, cols), lambda i: (0, i))
-        acc = pl.pallas_call(
-            functools.partial(token_first_kernel, scale, pair, early, local), grid=(steps,),
-            out_shape=sds((tok, hidden), F32),
-            in_specs=[full((8, tok)), col(u_early.shape[0]), col(tok), full((experts, tok)), col(experts)],
-            out_specs=col(tok), name='first',
-            cost_estimate=pl.CostEstimate(flops=4_000_000_000, bytes_accessed=8_000_000, transcendentals=0),
-            compiler_params=params())(meta, u_early, loss_probe, l_t, wr_t)
+        pick1, pick2 = pl.pallas_call(
+            functools.partial(pick_kernel, pair, early, local),
+            out_shape=[sds((tok, u_early.shape[0]), BF16), sds((tok, u_late.shape[0]), BF16)],
+            in_specs=[VMEM], out_specs=[VMEM] * 2, name='pick',
+            cost_estimate=pl.CostEstimate(flops=2_000_000_000, bytes_accessed=1_000_000, transcendentals=0),
+            compiler_params=params())(meta)
         d_tokens = pl.pallas_call(
-            functools.partial(token_last_kernel, pair, early, local), grid=(steps,),
+            functools.partial(token_kernel, scale), grid=(steps,),
             out_shape=sds((tok, hidden), BF16),
-            in_specs=[full((8, tok)), col(u_late.shape[0]), col(tok)],
-            out_specs=col(tok), name='last',
-            compiler_params=params())(meta, u_late, acc)
-
-        d_w_router = d_wr.transpose(0, 2, 1).reshape(hidden, experts)
+            in_specs=[full(pick1.shape), full(pick2.shape), col(u_early.shape[0]), col(u_late.shape[0]), col(tok),
+                      full((experts, tok)), col(experts)],
+            out_specs=col(tok), name='tokens',
+            compiler_params=params())(pick1, pick2, u_early, u_late, loss_probe, l_t, wr_t)
+
+        d_w_router = d_wr.T
         return loss[0, 0], d_tokens, d_w_in, d_w_out, d_w_router
 
     in_specs = (P('ep', None), P('ep'), P(None, None), P('ep', None, None), P('ep', None, None), P('ep', None))

time: 196 us -> 183 us (0.934)
  Pallas kernels: 190 us -> 173 us
  waiting for transfers between devices: 0.01 us -> 3.96 us
    pallas_call x1, Pallas kernels: 158 us -> 143 us  [local_step(): pl.pallas_call(functools.partial(layer_kernel, groups, capacity, scale, a...]
    all_to_all x1, waiting for transfers between devices: 0.01 us -> 3.96 us  [local_step(): lax.all_to_all(u_late, 'ep', 0, 0, tiled=True)]
    pallas_call x2, Pallas kernels: 11.7 us -> 8.98 us  [the longest x1 7.03 us: local_step(): pl.pallas_call(functools.partial(token_kernel, scale), grid=(steps,), out...]
  transfers between devices with their start and end apart: 1 -> 1, of which waited for: 0 -> 1; matrix products, arithmetic and copies ran while one was open for 1% -> 1% of each run, Pallas kernels for 14% -> 12%
where the time goes in v3:
time: 183 us
  Pallas kernels  173 us (95%)
  waiting for transfers between devices  3.96 us (2%)
  starting transfers between devices  3.19 us (2%)
  local copies, waits for them, and re-layouts  1.99 us (1%)
    pallas_call x1, Pallas kernels, local_step(): pl.pallas_call(functools.partial(layer_kernel, groups, capacity, scale, a...  143 us
    pallas_call x1, Pallas kernels, local_step(): pl.pallas_call(weight_kernel, grid=(local,), out_shape=[sds((local, hidde...  20.5 us
    pallas_call x1, Pallas kernels, local_step(): pl.pallas_call(functools.partial(token_kernel, scale), grid=(steps,), out...  7.03 us
    all_to_all x1, waiting for transfers between devices, local_step(): lax.all_to_all(u_late, 'ep', 0, 0, tiled=True)  3.96 us
  transfers between devices with their start and end apart: 1, of which 1 were waited for; matrix products, arithmetic and copies ran while one was open for 1% of the time, Pallas kernels for 12%

profile of v3, /device:TPU:0, one launch (start us, length us, event | category | flops | bytes accessed | tf_op | source)
XLA Modules:
  0.0 182.6 jit_solution(14595179959450695163)
XLA Ops:
  0.6 143.4 %layer.1 = (bf16[4,16,16,2048]{3,2,1,0:T(8,128)(2,1)}, bf16[4,256,1408]{2,1,0:T(8,128)(2,1)}, bf16[4,256,2048]{2,1,0:T(8,128)(2,1)}, bf16[4,256,1408]{2,1,0:T(8,...) custom-call(s32[1,512]{1,0:T(1,128)} %bitcast.11, ...), custom_call_target="tpu_custom_call" | custom-call | tf_op jit(solution)/shard_map/layer/pallas_call | solution.py:366
  144.0 3.2 %all-to-all-start = ((bf16[16,2,16,2048]{3,2,1,0:T(8,128)(2,1)}), bf16[16,2,16,2048]{3,2,1,0:T(8,128)(2,1)}, u32[]{:S(2)}, u32[]{:S(2)}) async-start(bf16[16,2,16,2048]{3,2,1,0:T(8,128)(2,1)} %get-tuple-element.24), calls=%async_computation | async-start | bytes 4194304 | tf_op jit(solution)/shard_map/all_to_all | solution.py:387
  147.2 1.2 slice.3
  148.4 2.0 %pick.1 = (bf16[512,512]{1,0:T(8,128)(2,1)}, bf16[512,512]{1,0:T(8,128)(2,1)}) custom-call(s32[8,512]{1,0:T(8,128)} %get-tuple-element.20.meta_ref), custom_call_target="tpu_custom_call" | custom-call | flops 2000000000 | bytes 1000000 | tf_op jit(solution)/shard_map/pick/pallas_call | solution.py:400
  150.4 20.5 %weights.1 = (bf16[4,2048,1408]{2,1,0:T(8,128)(2,1)}, bf16[4,1408,2048]{2,1,0:T(8,128)(2,1)}) custom-call(bf16[4,256,2048]{2,1,0:T(8,128)(2,1)} %bitcast.12, bf16[4,256,1408]{2,1,0:T(8,128)(2,1)} %get-tuple-element.27.h_ref, bf16[4,256,2048]{2,1,0:T(8,128)(2,1)} %get-tuple-element.28.g_ref, bf16[4,256,1408]{2,1,0:T(8,128)(2,1)} %get-tuple-element.29.q_ref), custom_call_target="tpu_custom_call" | custom-call | flops 11811160064 | bytes 50000000 | tf_op jit(solution)/shard_map/weights/pallas_call | solution.py:390
  170.8 4.0 %all-to-all-done = bf16[16,2,16,2048]{3,2,1,0:T(8,128)(2,1)} async-done(((bf16[16,2,16,2048]{3,2,1,0:T(8,128)(2,1)}), bf16[16,2,16,2048]{3,2,1,0:T(8,128)(2,1)}, u32[]{:S(2)}, u32[]{:S(2)}) %all-to-all-start) | async-done | bytes 2097184 | tf_op jit(solution)/shard_map/all_to_all | solution.py:387
  174.8 0.0 copy-start
  174.8 7.0 %tokens.1 = bf16[512,2048]{1,0:T(8,128)(2,1)} custom-call(bf16[512,512]{1,0:T(8,128)(2,1)} %get-tuple-element.21.pick1_ref, bf16[512,512]{1,0:T(8,128)(2,1)} %get-tuple-element.22.pick2_ref, bf16[512,2048]{1,0:T(8,128)(2,1)} %bitcast.7, bf16[512,2048]{1,0:T(8,128)(2,1)} %bitcast.4.u2_ref, bf16[512,2048]{1,0:T(8,128)(2,1)} %r_ref.3, ...), custom_call_target="tpu_custom_call" | custom-call | tf_op jit(solution)/shard_map/tokens/pallas_call | solution.py:406
  181.8 0.0 copy-done
  181.8 0.8 copy.12
Async XLA Ops:
  144.0 30.8 %all-to-all-start = ((bf16[16,2,16,2048]{3,2,1,0:T(8,128)(2,1)}), bf16[16,2,16,2048]{3,2,1,0:T(8,128)(2,1)}, u32[]{:S(2)}, u32[]{:S(2)}) async-start(bf16[16,2,16,2048]{3,2,1,0:T(8,128)(2,1)} %get-tuple-element.24), calls=%async_computation | async-start | bytes 4194304 | tf_op jit(solution)/shard_map/all_to_all | solution.py:387
  174.8 7.0 %copy-start = (f32[64,2048]{1,0:T(8,128)S(1)}, f32[64,2048]{1,0:T(8,128)}, u32[]{:S(2)}) copy-start(f32[64,2048]{1,0:T(8,128)} %get-tuple-element.32) | copy-start | bytes 1572868
